TPU v7x, 32 devices: a 4x4x1 block of a 4x4x8 slice. The times are simulated.
32 devices in a mesh: dp: 1 (over z), tp: 4 (over y), sp: 8 (over x, core).
Axes of the slice: x: 4, y: 4, z: 1, core: 2. Of those that a mesh axis runs over, the one named last changes fastest.
The devices are a block of a 4x4x8 slice.
Arguments:
- x_in: bfloat16 [128, 5376], P('dp')
- cur_pos: int32 [128], P('dp')
- w_pre: float32 [5376], replicated
- w_q: bfloat16 [5376, 4096], P(None, 'tp')
- w_k: bfloat16 [5376, 2048], P(None, 'tp')
- w_v: bfloat16 [5376, 2048], P(None, 'tp')
- w_o: bfloat16 [4096, 5376], P('tp')
- w_post: float32 [5376], replicated
- k_cache: bfloat16 [128, 512, 16, 128], P('dp', 'sp', 'tp')
- v_cache: bfloat16 [128, 512, 16, 128], P('dp', 'sp', 'tp')
Outputs:
- output 1: bfloat16 [128, 5376], P('dp')
- output 2: bfloat16 [128, 512, 16, 128], P('dp', 'sp', 'tp')
- output 3: bfloat16 [128, 512, 16, 128], P('dp', 'sp', 'tp')
All inputs are finite; a program needn't handle non-finite values.
Results may differ from a plain program's by a relative error of at most 0.00624945.
Values sent between devices are 32-bit elements.
A program may use at most 768 MiB of HBM per device.

v0:
```python
import jax
import jax.numpy as jnp
from jax import lax
from jax.sharding import PartitionSpec as P

SOFT_CAP = 50.0
ROPE_BASE = 10000.0
NORM_EPS = 1e-6
NEG_FILL = -1e30


def rms_scale(tensor, gain_w):
    mean_sq = jnp.mean(tensor * tensor, axis=-1, keepdims=True)
    return tensor * lax.rsqrt(mean_sq + NORM_EPS) * (1.0 + gain_w)


def rotary(tensor, positions):
    half_dim = tensor.shape[-1] // 2
    inv_freq = ROPE_BASE ** (-2.0 * jnp.arange(half_dim, dtype=jnp.float32) / (2 * half_dim))
    angles = positions.astype(jnp.float32)[:, None] * inv_freq[None, :]
    angles = angles.reshape((angles.shape[0],) + (1,) * (tensor.ndim - 2) + (half_dim,))
    cos_tab = jnp.cos(angles)
    sin_tab = jnp.sin(angles)
    lo_half = tensor[..., :half_dim]
    hi_half = tensor[..., half_dim:]
    return jnp.concatenate([lo_half * cos_tab - hi_half * sin_tab, hi_half * cos_tab + lo_half * sin_tab], axis=-1)


def solution(mesh):
    cache_spec = P('dp', 'sp', 'tp', None)

    def local_step(x_in, cur_pos, w_pre, w_q, w_k, w_v, w_o, w_post, k_cache, v_cache):
        row_count, seq_block, kv_local, head_dim = k_cache.shape
        heads_local = w_q.shape[1] // head_dim
        group_size = heads_local // kv_local
        sp_index = lax.axis_index('sp')
        normed = rms_scale(x_in.astype(jnp.float32), w_pre).astype(jnp.bfloat16)
        q_proj = jnp.dot(normed, w_q, preferred_element_type=jnp.float32)
        q_rot = rotary(q_proj.reshape(row_count, kv_local, group_size, head_dim), cur_pos).astype(jnp.bfloat16)
        k_proj = jnp.dot(normed, w_k, preferred_element_type=jnp.float32)
        k_new = rotary(k_proj.reshape(row_count, kv_local, head_dim), cur_pos).astype(jnp.bfloat16)
        v_new = jnp.dot(normed, w_v, preferred_element_type=jnp.float32).reshape(row_count, kv_local, head_dim).astype(jnp.bfloat16)
        block_pos = sp_index * seq_block + jnp.arange(seq_block)
        slot_hit = (block_pos[None, :] == cur_pos[:, None])[:, :, None, None]
        k_out = jnp.where(slot_hit, k_new[:, None], k_cache)
        v_out = jnp.where(slot_hit, v_new[:, None], v_cache)
        raw_score = jnp.einsum('bgrd,btgd->bgrt', q_rot, k_out, preferred_element_type=jnp.float32)
        capped = SOFT_CAP * jnp.tanh(raw_score * (head_dim ** -0.5 / SOFT_CAP))
        is_valid = (block_pos[None, :] <= cur_pos[:, None])[:, None, None, :]
        capped = jnp.where(is_valid, capped, NEG_FILL)
        block_max = jnp.max(capped, axis=-1)
        exp_w = jnp.where(is_valid, jnp.exp(capped - block_max[..., None]), 0.0)
        block_sum = jnp.sum(exp_w, axis=-1)
        block_out = jnp.einsum('bgrt,btgd->bgrd', exp_w.astype(jnp.bfloat16), v_out, preferred_element_type=jnp.float32)
        global_max = lax.pmax(block_max, 'sp')
        factor = jnp.exp(block_max - global_max)
        packed = jnp.concatenate([block_out * factor[..., None], (block_sum * factor)[..., None]], axis=-1)
        merged = lax.psum(packed, 'sp')
        attn_out = (merged[..., :head_dim] / merged[..., head_dim:]).reshape(row_count, heads_local * head_dim)
        proj_part = jnp.dot(attn_out.astype(jnp.bfloat16), w_o, preferred_element_type=jnp.float32)
        proj_sum = lax.psum(proj_part, 'tp')
        x_out = (x_in.astype(jnp.float32) + rms_scale(proj_sum, w_post)).astype(jnp.bfloat16)
        return x_out, k_out, v_out

    return jax.shard_map(local_step, mesh=mesh,
                         in_specs=(P('dp', None), P('dp'), P(None), P(None, 'tp'), P(None, 'tp'), P(None, 'tp'), P('tp', None), P(None), cache_spec, cache_spec),
                         out_specs=(P('dp', None), cache_spec, cache_spec), check_vma=False)
```

profile of v0, /device:TPU:97, one launch (start us, length us, event | category | flops | bytes accessed | tf_op | source)
XLA Modules:
  0.0 232.4 jit_solution(5343313603646978660)
XLA Ops:
  7.3 0.7 broadcast_add_fusion.1
  8.0 1.7 fusion.4
  9.7 4.0 %fusion.32 = f32[128,512]{1,0:T(8,128)S(1)} fusion(bf16[5376,512]{1,0:T(8,128)(2,1)} %param.14, bf16[128,5376]{1,0:T(8,128)(2,1)} %param.10, f32[5376]{0:T(1024)S(1)} %broadcast_add_fusion.1, f32[128]{0:T(128)S(1)} %add_rsqrt_fusion.1), kind=kOutput, calls=%fused_computation.48 | convolution fusion | flops 707395584 | bytes 7165440 | tf_op jit(solution)/shard_map/dot_general | solution.py:40
  13.9 3.5 %convolution_convert_fusion = bf16[128,512]{1,0:T(8,128)(2,1)S(1)} fusion(bf16[5376,512]{1,0:T(8,128)(2,1)} %param.15, bf16[128,5376]{1,0:T(8,128)(2,1)S(1)} %copy-done, f32[5376]{0:T(1024)S(1)} %broadcast_add_fusion.1, f32[128]{0:T(128)S(1)} %add_rsqrt_fusion.1), kind=kOutput, calls=%fused_computation.18 | convolution fusion | flops 707461120 | bytes 7034368 | tf_op jit(solution)/shard_map/dot_general | solution.py:42
  17.5 5.8 %fusion.34 = f32[128,1024]{1,0:T(8,128)S(1)} fusion(bf16[5376,1024]{1,0:T(8,128)(2,1)} %param.13, bf16[128,5376]{1,0:T(8,128)(2,1)S(1)} %copy-done, f32[5376]{0:T(1024)S(1)} %broadcast_add_fusion.1, f32[128]{0:T(128)S(1)} %add_rsqrt_fusion.1), kind=kOutput, calls=%fused_computation.49 | convolution fusion | flops 1412038656 | bytes 12932608 | tf_op jit(solution)/shard_map/dot_general | solution.py:38
  23.3 0.4 reshape.208
  24.4 0.8 subtract_convert_fusion
  25.4 14.2 %broadcast_select_fusion = (bf16[128,64,4,128]{3,2,1,0:T(4,128)(2,1)}, bf16[128,64,4,128]{3,2,1,0:T(4,128)(2,1)S(1)}) fusion(bf16[128,64,4,128]{3,2,1,0:T(4,128)(2,1)} %param.19, pred[128,64]{1,0:T(8,128)(4,1)S(1)} %get-tuple-element.12, bf16[128,4,128]{2,1,0:T(4,128)(2,1)S(1)} %convert_element_type.44, bf16[128,64,4,128]{3,2,1,0:T(4,128)(2,1)} %param.18, ...), kind=kLoop, calls=%fused_computation.4 | loop fusion | flops 8388608 | bytes 33824768 | tf_op jit(solution)/shard_map/jit(_where)/select_n | solution.py:46
  39.6 4.9 %fusion.36 = (f32[128,4,2]{2,1,0:T(4,128)S(1)}, f32[128,4,2,64]{3,2,1,0:T(2,128)S(1)}) fusion(bf16[128,64,4,128]{3,2,1,0:T(4,128)(2,1)S(1)} %get-tuple-element.10, bf16[128,4,2,64]{3,2,1,0:T(2,128)(2,1)S(1)} %get-tuple-element.6, bf16[128,4,2,64]{3,2,1,0:T(2,128)(2,1)S(1)} %get-tuple-element.5, pred[128,64]{1,0:T(8,128)(4,1)S(1)} %get-tuple-element.11), kind=kOutput, calls=%fused_computation.50 | convolution fusion | flops 17562624 | bytes 8925184 | tf_op jit(solution)/shard_map/bgrd,btgd->bgrt/dot_general | solution.py:47
  44.6 26.9 %pmax.7 = f32[128,4,2]{2,1,0:T(4,128)S(1)} all-reduce(f32[128,4,2]{2,1,0:T(4,128)S(1)} %get-tuple-element.15), channel_id=1, replica_groups=mesh['dp'=1,'tp'=4,'sp'=8] {'sp'}, use_global_device_ids=true, to_apply=%region_2.3 | all-reduce | flops 1024 | bytes 8192 | tf_op jit(solution)/shard_map/pmax | solution.py:55
  71.5 1.4 fusion.28
  73.0 3.2 %copy.25 = f32[128,4,2,1]{3,2,1,0:T(2,128)S(1)} copy(f32[128,4,2,1]{2,1,0,3:T(4,128)S(1)} %get-tuple-element.3) | data formatting | bytes 8192 | tf_op jit(solution)/shard_map/broadcast_in_dim | solution.py:57
  76.2 5.9 %fusion.17 = f32[128,4,2,128]{3,2,1,0:T(2,128)S(1)} fusion(bf16[128,64,4,128]{3,2,1,0:T(4,128)(2,1)} %get-tuple-element.9, f32[128,4,2]{2,1,0:T(4,128)S(1)} %get-tuple-element.4, f32[128,4,2,64]{3,2,1,0:T(2,128)S(1)} %get-tuple-element.16, pred[128,64]{1,0:T(8,128)(4,1)S(1)} %get-tuple-element.11, f32[128,4,2]{2,1,0:T(4,128)S(1)} %get-tuple-element.15), kind=kOutput, calls=%fused_computation.17 | convolution fusion | flops 17104896 | bytes 9191424 | tf_op jit(solution)/shard_map/bgrt,btgd->bgrd/dot_general | solution.py:54
  82.2 1.5 pad_maximum_fusion
  83.8 58.8 %all-reduce.3.cloned.1.call-done = f32[128,4,2,129]{3,2,1,0:T(2,128)} async-done(((f32[128,4,2,129]{3,2,1,0:T(2,128)}), f32[128,4,2,129]{3,2,1,0:T(2,128)}) %all-reduce.3.cloned.1.call-update) | async-done | bytes 528400 | tf_op jit(solution)/shard_map/psum | solution.py:58
  142.6 1.1 slice.29
  143.7 3.1 %copy.30 = f32[128,4,2,1]{2,1,0,3:T(4,128)S(1)} copy(f32[128,4,2,1]{3,2,1,0:T(2,128)S(1)} %slice.29) | data formatting | bytes 8192 | tf_op jit(solution)/shard_map/div | solution.py:59
  146.8 1.7 fusion.23
  148.7 7.3 %fusion.37 = f32[128,5376]{1,0:T(8,128)} fusion(bf16[128,1024]{1,0:T(8,128)(2,1)S(1)} %convert_element_type.46, bf16[1024,5376]{1,0:T(8,128)(2,1)} %param.16), kind=kOutput, calls=%fused_computation.51 | convolution fusion | flops 1409286144 | bytes 14024704 | tf_op jit(solution)/shard_map/dot_general | solution.py:60
  156.1 0.7 copy-done.3
  156.7 64.7 %all-reduce.5.cloned.1.call-done = f32[128,5376]{1,0:T(8,128)} async-done(((f32[128,5376]{1,0:T(8,128)}), f32[128,5376]{1,0:T(8,128)}) %all-reduce.5.cloned.1.call-update) | async-done | bytes 2752528 | tf_op jit(solution)/shard_map/psum | solution.py:61
  221.4 2.2 multiply_reduce_fusion
  223.6 0.4 copy-done.1
  224.0 1.6 fusion.7
  (26 shorter events, 1.6 us)
Async XLA Ops:
  7.2 135.4 %all-reduce.3.cloned.1.call-start = ((), (), s32[]{:S(2)}) async-start(), calls=%async_computation | async-start | bytes 2097152 | tf_op jit(solution)/shard_map/psum | solution.py:58
  9.7 4.1 %copy-start.4 = (s32[128]{0:T(128)S(1)}, s32[128]{0:T(128)}, u32[]{:S(2)}) copy-start(s32[128]{0:T(128)} %param.11) | copy-start | bytes 1540
  9.7 4.1 %copy-start = (bf16[128,5376]{1,0:T(8,128)(2,1)S(1)}, bf16[128,5376]{1,0:T(8,128)(2,1)}, u32[]{:S(2)}) copy-start(bf16[128,5376]{1,0:T(8,128)(2,1)} %param.10) | copy-start | bytes 4128772
  39.6 4.9 %copy-start.2 = (bf16[128,64,4,128]{3,2,1,0:T(4,128)(2,1)}, bf16[128,64,4,128]{3,2,1,0:T(4,128)(2,1)S(1)}, u32[]{:S(2)}) copy-start(bf16[128,64,4,128]{3,2,1,0:T(4,128)(2,1)S(1)} %get-tuple-element.10) | copy-start | bytes 25165828
  83.7 137.7 %all-reduce.5.cloned.1.call-start = ((), (), s32[]{:S(2)}) async-start(), calls=%async_computation.1 | async-start | bytes 5505024 | tf_op jit(solution)/shard_map/psum | solution.py:61
  156.0 0.7 copy-start.3
  221.4 2.6 %copy-start.1 = (f32[128,5376]{1,0:T(8,128)S(1)}, f32[128,5376]{1,0:T(8,128)}, u32[]{:S(2)}) copy-start(f32[128,5376]{1,0:T(8,128)} %all-reduce.5.cloned.1.call-done) | copy-start | bytes 8257540
Sparse Core Ops, SparseCore 0:
  83.8 58.7 all-reduce.2
  156.2 65.1 all-reduce.4
where the time goes:
time: 233 us; the launch traced here: 232 us
  waiting for transfers between devices  124 us (53%)
  matrix products  31.4 us (13%)
  other arithmetic  26.9 us (12%)
  blocking collectives  26.9 us (12%)
  between operations  14.3 us (6%)
  local copies, waits for them, and re-layouts  9.26 us (4%)
    psum x1, waiting for transfers between devices, local_step(): proj_sum = lax.psum(proj_part, 'tp')  64.7 us
    psum x1, waiting for transfers between devices, local_step(): merged = lax.psum(packed, 'sp')  58.8 us
    pmax x1, blocking collectives, local_step(): global_max = lax.pmax(block_max, 'sp')  26.9 us
    select_n x1, other arithmetic, local_step(): v_out = jnp.where(slot_hit, v_new[:, None], v_cache)  14.2 us
    dot_general x1, matrix products, local_step(): jnp.dot(attn_out.astype(jnp.bfloat16), w_o, preferred_element_type=jnp.fl...  7.31 us
    dot_general x1, matrix products, local_step(): jnp.einsum('bgrt,btgd->bgrd', exp_w.astype(jnp.bfloat16), v_out, preferre...  5.93 us
    dot_general x1, matrix products, local_step(): q_proj = jnp.dot(normed, w_q, preferred_element_type=jnp.float32)  5.76 us
    dot_general x1, matrix products, local_step(): jnp.einsum('bgrd,btgd->bgrt', q_rot, k_out, preferred_element_type=jnp.fl...  4.93 us
  transfers between devices with their start and end apart: 2, of which 2 were waited for; matrix products, arithmetic and copies ran while one was open for 0% of the time, Pallas kernels for 0%

commit v1 on v0

--- a/solution.py
+++ b/solution.py
@@ -1,12 +1,18 @@
+import functools
+
 import jax
 import jax.numpy as jnp
 from jax import lax
+from jax.experimental import pallas as pl
+from jax.experimental.pallas import tpu as pltpu
 from jax.sharding import PartitionSpec as P
 
 SOFT_CAP = 50.0
 ROPE_BASE = 10000.0
 NORM_EPS = 1e-6
 NEG_FILL = -1e30
+MESH = pl.DeviceIdType.MESH
+RING = 4
 
 
 def rms_scale(tensor, gain_w):
@@ -26,8 +32,304 @@
     return jnp.concatenate([lo_half * cos_tab - hi_half * sin_tab, hi_half * cos_tab + lo_half * sin_tab], axis=-1)
 
 
+FIRST_P, FIRST_M, DIAG_A, DIAG_B = 0, 1, 2, 3
+UNITS = ('own', 'prev', 'next', 'diag_a', 'diag_b')
+SECOND = {(u, d): 4 + 2 * i + j for i, u in enumerate(UNITS) for j, d in enumerate((1, -1))}
+FORWARD = {u: 14 + i for i, u in enumerate(('own_a', 'own_b', 'prev', 'next', 'diag_a', 'diag_b'))}
+N_GATHER = 20
+
+
+def comm_kernel(heads, o_ref, wo_hbm, x_hbm, wpost_ref, out_ref,
+                wo_v, x_v, pair_r, comb, sp_r, scr, part, tp_r, gath,
+                wo_sem, x_sem, pair_ss, pair_rs, sp_ss, sp_rs, tp_ss, tp_rs, ag_ss, ag_rs, dd_ss, dd_rs):
+    y = lax.axis_index('tp')
+    s = lax.axis_index('sp')
+    xc = s // 2
+    c = s % 2
+    slab_rows, dim = comb.shape[1], comb.shape[2]
+    row_block = (slab_rows - 2 * heads) // heads
+    sub = row_block // RING
+    width = part.shape[2]
+    stat = row_block * heads
+
+    def chip(dx, dy):
+        return {'tp': (y + dy) % RING, 'sp': ((xc + dx) % RING) * 2 + c}
+
+    partner = {'sp': xc * 2 + (1 - c)}
+
+    barrier = pltpu.get_barrier_semaphore()
+    pl.semaphore_signal(barrier, inc=1, device_id=partner, device_id_type=MESH)
+    for k in range(1, RING):
+        pl.semaphore_signal(barrier, inc=1, device_id=chip(k, 0), device_id_type=MESH)
+        pl.semaphore_signal(barrier, inc=1, device_id=chip(0, k), device_id_type=MESH)
+
+    wo_rows = wo_v.shape[0] // RING
+    wo_copies = []
+    for i in range(RING):
+        rows = pl.ds(i * wo_rows, wo_rows)
+        wo_copies.append(pltpu.make_async_copy(wo_hbm.at[rows], wo_v.at[rows], wo_sem.at[i]))
+        wo_copies[-1].start()
+    x_copy = pltpu.make_async_copy(x_hbm.at[pl.ds(pl.multiple_of(s * row_block, row_block), row_block)], x_v, x_sem)
+    x_copy.start()
+
+    pl.semaphore_wait(barrier, 2 * RING - 1)
+
+    order = (2, 1, 3, 0)
+    pair = []
+    for k in order:
+        there = (xc + k) % RING
+        pair.append(pltpu.make_async_remote_copy(
+            src_ref=o_ref.at[(1 - c) * RING + there], dst_ref=pair_r.at[there],
+            send_sem=pair_ss.at[k], recv_sem=pair_rs.at[k], device_id=partner, device_id_type=MESH))
+        pair[-1].start()
+    sp_copies = {}
+    for i, k in enumerate(order):
+        there = (xc + k) % RING
+        mine = c * RING + there
+        pair[i].wait_recv()
+        m0 = o_ref[mine, pl.ds(stat, heads), :]
+        l0 = o_ref[mine, pl.ds(stat + heads, heads), :]
+        m1 = pair_r[there, pl.ds(stat, heads), :]
+        l1 = pair_r[there, pl.ds(stat + heads, heads), :]
+        top = jnp.maximum(m0, m1)
+        f0 = jnp.exp(m0 - top)
+        f1 = jnp.exp(m1 - top)
+        comb[there, pl.ds(stat, heads), :] = top
+        comb[there, pl.ds(stat + heads, heads), :] = l0 * f0 + l1 * f1
+        for j in range(row_block):
+            rows = pl.ds(j * heads, heads)
+            comb[there, rows, :] = o_ref[mine, rows, :] * f0[:, j:j + 1] + pair_r[there, rows, :] * f1[:, j:j + 1]
+        if k:
+            sp_copies[k] = pltpu.make_async_remote_copy(
+                src_ref=comb.at[there], dst_ref=sp_r.at[RING - k - 1],
+                send_sem=sp_ss.at[k - 1], recv_sem=sp_rs.at[RING - k - 1], device_id=chip(k, 0), device_id_type=MESH)
+            sp_copies[k].start()
+
+    def arrived(k):
+        return pltpu.make_async_remote_copy(
+            src_ref=comb.at[xc], dst_ref=sp_r.at[k - 1], send_sem=sp_ss.at[k - 1], recv_sem=sp_rs.at[k - 1],
+            device_id=chip(k, 0), device_id_type=MESH)
+    for k in (1, 3, 2):
+        arrived(k).wait_recv()
+    m_all = [comb[xc, pl.ds(stat, heads), :]] + [sp_r[k, pl.ds(stat, heads), :] for k in range(RING - 1)]
+    l_all = [comb[xc, pl.ds(stat + heads, heads), :]] + [sp_r[k, pl.ds(stat + heads, heads), :] for k in range(RING - 1)]
+    top = functools.reduce(jnp.maximum, m_all)
+    f_all = [jnp.exp(m - top) for m in m_all]
+    total = sum(l * f for l, f in zip(l_all, f_all))
+    lane = lax.broadcasted_iota(jnp.int32, total.shape, 1)
+    inv = 1.0 / jnp.where(lane < row_block, total, 1.0)
+    f_all = [f * inv for f in f_all]
+    for j in range(row_block):
+        rows = pl.ds(j * heads, heads)
+        acc = comb[xc, rows, :] * f_all[0][:, j:j + 1]
+        for k in range(RING - 1):
+            acc += sp_r[k, rows, :] * f_all[k + 1][:, j:j + 1]
+        scr[rows, :] = acc
+    attn = jnp.concatenate([scr[pl.ds(h, row_block, stride=heads), :].astype(jnp.bfloat16) for h in range(heads)], axis=1)
+
+    for copy in wo_copies:
+        copy.wait()
+    n_chunk = tp_ss.shape[0] // (RING - 1)
+    cols = width // n_chunk
+    tp_copies = []
+    for n in range(n_chunk):
+        span = pl.ds(n * cols, cols)
+        prod = jnp.dot(attn, wo_v[:, span], preferred_element_type=jnp.float32)
+        for t in range(RING):
+            part[t, :, span] = prod[t * sub:(t + 1) * sub]
+        for k in (2, 1, 3):
+            to = (y + k) % RING
+            copy = pltpu.make_async_remote_copy(
+                src_ref=part.at[to, :, span], dst_ref=tp_r.at[RING - k - 1, :, span],
+                send_sem=tp_ss.at[n * (RING - 1) + k - 1], recv_sem=tp_rs.at[n * (RING - 1) + RING - k - 1],
+                device_id=chip(0, k), device_id_type=MESH)
+            copy.start()
+            tp_copies.append(copy)
+    x_copy.wait()
+    for copy in tp_copies:
+        copy.wait_recv()
+    ssq = jnp.zeros((sub, 1), jnp.float32)
+    u_all = []
+    for n in range(n_chunk):
+        span = pl.ds(n * cols, cols)
+        u = part[y, :, span]
+        for k in range(RING - 1):
+            u += tp_r[k, :, span]
+        ssq += jnp.sum(u * u, axis=1, keepdims=True)
+        u_all.append(u)
+    scale = lax.rsqrt(ssq / width + NORM_EPS)
+
+    a, b = xc * (1 - c) + y * c, y * (1 - c) + xc * c
+
+    def place(da, db):
+        return c * RING * RING + ((a + da) % RING) * RING + (b + db) % RING
+
+    for n in range(n_chunk):
+        span = pl.ds(n * cols, cols)
+        x16 = x_v[:, span].astype(jnp.float32)
+        x4 = x16[0:sub]
+        for t in range(1, RING):
+            x4 = jnp.where(y == t, x16[t * sub:(t + 1) * sub], x4)
+        gath[place(0, 0), :, span] = x4 + u_all[n] * scale * (1.0 + wpost_ref[:, span])
+
+    def device(da, db):
+        return chip(da * (1 - c) + db * c, db * (1 - c) + da * c)
+
+    half = width // 2
+    parts = {'': pl.ds(0, width), 'a': pl.ds(0, half), 'b': pl.ds(half, half)}
+
+    def message(src, part_key, to, number):
+        ref = gath.at[place(*src), :, parts[part_key]]
+        return pltpu.make_async_remote_copy(
+            src_ref=ref, dst_ref=ref, send_sem=ag_ss.at[number], recv_sem=ag_rs.at[number],
+            device_id=device(*to), device_id_type=MESH)
+
+    sent = []
+
+    def send(*args):
+        copy = message(*args)
+        copy.start()
+        sent.append(copy)
+
+    def wait(src, part_key, number):
+        message(src, part_key, (0, 0), number).wait_recv()
+
+    def to_pair(da, db):
+        ref = gath.at[place(da, db)]
+        number = da % RING * RING + db % RING
+        copy = pltpu.make_async_remote_copy(
+            src_ref=ref, dst_ref=ref, send_sem=dd_ss.at[number], recv_sem=dd_rs.at[number],
+            device_id=partner, device_id_type=MESH)
+        copy.start()
+        sent.append(copy)
+
+    unit = {'own': (0, ''), 'prev': (-1, ''), 'next': (1, ''), 'diag_a': (2, 'a'), 'diag_b': (2, 'b')}
+
+    def second(name):
+        da, key = unit[name]
+        for d in (1, -1):
+            send((da, 0), key, (0, d), SECOND[name, d])
+
+    def got_second(name, d):
+        da, key = unit[name]
+        wait((da, -d), key, SECOND[name, d])
+
+    def forward(da, d, key, name):
+        send((da, -d), key, (0, d), FORWARD[name])
+
+    send((0, 0), '', (1, 0), FIRST_P)
+    send((0, 0), '', (-1, 0), FIRST_M)
+    second('own')
+    to_pair(0, 0)
+    wait((-1, 0), '', FIRST_P)
+    send((-1, 0), 'a', (1, 0), DIAG_A)
+    second('prev')
+    to_pair(-1, 0)
+    wait((1, 0), '', FIRST_M)
+    send((1, 0), 'b', (-1, 0), DIAG_B)
+    second('next')
+    to_pair(1, 0)
+    got_second('own', 1)
+    forward(0, 1, 'a', 'own_a')
+    to_pair(0, -1)
+    got_second('own', -1)
+    forward(0, -1, 'b', 'own_b')
+    to_pair(0, 1)
+    wait((2, 0), 'a', DIAG_A)
+    second('diag_a')
+    wait((2, 0), 'b', DIAG_B)
+    second('diag_b')
+    to_pair(2, 0)
+    got_second('prev', 1)
+    forward(-1, 1, '', 'prev')
+    to_pair(-1, -1)
+    got_second('next', -1)
+    forward(1, -1, '', 'next')
+    to_pair(1, 1)
+    got_second('prev', -1)
+    to_pair(-1, 1)
+    got_second('next', 1)
+    to_pair(1, -1)
+    wait((0, 2), 'a', FORWARD['own_a'])
+    wait((0, 2), 'b', FORWARD['own_b'])
+    to_pair(0, 2)
+    got_second('diag_a', 1)
+    forward(2, 1, 'a', 'diag_a')
+    got_second('diag_b', -1)
+    forward(2, -1, 'b', 'diag_b')
+    got_second('diag_b', 1)
+    to_pair(2, -1)
+    got_second('diag_a', -1)
+    to_pair(2, 1)
+    wait((-1, 2), '', FORWARD['prev'])
+    to_pair(-1, 2)
+    wait((1, 2), '', FORWARD['next'])
+    to_pair(1, 2)
+    wait((2, 2), 'a', FORWARD['diag_a'])
+    wait((2, 2), 'b', FORWARD['diag_b'])
+    to_pair(2, 2)
+
+    a2, b2 = b, a
+    for da in range(RING):
+        for db in range(RING):
+            ref = gath.at[(1 - c) * RING * RING + ((a2 + da) % RING) * RING + (b2 + db) % RING]
+            pltpu.make_async_remote_copy(
+                src_ref=ref, dst_ref=ref, send_sem=dd_ss.at[da * RING + db], recv_sem=dd_rs.at[da * RING + db],
+                device_id=partner, device_id_type=MESH).wait_recv()
+
+    for cx in range(RING):
+        for cc in range(2):
+            rows = pl.ds((2 * cx + cc) * row_block, row_block)
+            for n in range(n_chunk):
+                span = pl.ds(n * cols, cols)
+                blocks = [gath[cx * RING + t if cc == 0 else RING * RING + t * RING + cx, :, span] for t in range(RING)]
+                out_ref[rows, span] = jnp.concatenate(blocks, axis=0).astype(out_ref.dtype)
+
+    for copy in pair:
+        copy.wait_send()
+    for copy in list(sp_copies.values()) + tp_copies + sent:
+        copy.wait_send()
+
+
+def finish(o_pack, w_o, x_in, w_post, heads):
+    rows, width = x_in.shape
+    _, slab_rows, dim = o_pack.shape
+    row_block = rows // (2 * RING)
+    n_chunk = 3 if width % (3 * 256) == 0 else 1
+    sems = pltpu.SemaphoreType.DMA
+    vmem = pl.BlockSpec(memory_space=pltpu.VMEM)
+    return pl.pallas_call(
+        functools.partial(comm_kernel, heads),
+        out_shape=jax.ShapeDtypeStruct((rows, width), x_in.dtype),
+        in_specs=[vmem, pl.BlockSpec(memory_space=pl.ANY), pl.BlockSpec(memory_space=pl.ANY), vmem],
+        out_specs=vmem,
+        scratch_shapes=[
+            pltpu.VMEM(w_o.shape, w_o.dtype),
+            pltpu.VMEM((row_block, width), x_in.dtype),
+            pltpu.VMEM((RING, slab_rows, dim), jnp.float32),
+            pltpu.VMEM((RING, slab_rows, dim), jnp.float32),
+            pltpu.VMEM((RING - 1, slab_rows, dim), jnp.float32),
+            pltpu.VMEM((row_block * heads, dim), jnp.float32),
+            pltpu.VMEM((RING, row_block // RING, width), jnp.float32),
+            pltpu.VMEM((RING - 1, row_block // RING, width), jnp.float32),
+            pltpu.VMEM((2 * RING * RING, row_block // RING, width), jnp.float32),
+            sems((RING,)), sems(()),
+            sems((RING,)), sems((RING,)),
+            sems((RING - 1,)), sems((RING - 1,)),
+            sems((n_chunk * (RING - 1),)), sems((n_chunk * (RING - 1),)),
+            sems((N_GATHER,)), sems((N_GATHER,)),
+            sems((RING * RING,)), sems((RING * RING,)),
+        ],
+        compiler_params=pltpu.CompilerParams(collective_id=0, has_side_effects=True, vmem_limit_bytes=40 * 2**20),
+        cost_estimate=pl.CostEstimate(flops=2 * rows * w_o.size // 8, bytes_accessed=w_o.size * 2, transcendentals=0),
+        name='finish',
+    )(o_pack, w_o, x_in, w_post[None])
+
+
 def solution(mesh):
     cache_spec = P('dp', 'sp', 'tp', None)
+    n_sp = mesh.shape['sp']
+    assert n_sp == 2 * RING and mesh.shape['tp'] == RING
 
     def local_step(x_in, cur_pos, w_pre, w_q, w_k, w_v, w_o, w_post, k_cache, v_cache):
         row_count, seq_block, kv_local, head_dim = k_cache.shape
@@ -52,14 +354,16 @@
         exp_w = jnp.where(is_valid, jnp.exp(capped - block_max[..., None]), 0.0)
         block_sum = jnp.sum(exp_w, axis=-1)
         block_out = jnp.einsum('bgrt,btgd->bgrd', exp_w.astype(jnp.bfloat16), v_out, preferred_element_type=jnp.float32)
-        global_max = lax.pmax(block_max, 'sp')
-        factor = jnp.exp(block_max - global_max)
-        packed = jnp.concatenate([block_out * factor[..., None], (block_sum * factor)[..., None]], axis=-1)
-        merged = lax.psum(packed, 'sp')
-        attn_out = (merged[..., :head_dim] / merged[..., head_dim:]).reshape(row_count, heads_local * head_dim)
-        proj_part = jnp.dot(attn_out.astype(jnp.bfloat16), w_o, preferred_element_type=jnp.float32)
-        proj_sum = lax.psum(proj_part, 'tp')
-        x_out = (x_in.astype(jnp.float32) + rms_scale(proj_sum, w_post)).astype(jnp.bfloat16)
+
+        row_block = row_count // n_sp
+
+        def stat_tile(t):
+            t = t.reshape(n_sp, row_block, heads_local).transpose(0, 2, 1)
+            return jnp.pad(t, ((0, 0), (0, 0), (0, head_dim - row_block)))
+
+        slabs = jnp.concatenate([block_out.reshape(n_sp, row_block * heads_local, head_dim), stat_tile(block_max), stat_tile(block_sum)], axis=1)
+        slabs = slabs.reshape(RING, 2, *slabs.shape[1:]).transpose(1, 0, 2, 3).reshape(slabs.shape)
+        x_out = finish(slabs, w_o, x_in, w_post, heads_local)
         return x_out, k_out, v_out
 
     return jax.shard_map(local_step, mesh=mesh,

time: 233 us -> 90.7 us (0.39)
  waiting for transfers between devices: 124 us -> 0 us
  Pallas kernels: 0 us -> 37 us
  blocking collectives: 26.9 us -> 0 us
  between operations: 14.3 us -> 0.83 us
  matrix products: 31.4 us -> 24.1 us
  other arithmetic: 26.9 us -> 21.3 us
    psum x2 -> x0, waiting for transfers between devices: 123 us -> none  [the longest x1 64.7 us: local_step(): proj_sum = lax.psum(proj_part, 'tp')]
    pallas_call x0 -> x1, Pallas kernels: none -> 37 us  [finish(): pl.pallas_call(functools.partial(comm_kernel, heads), out_shape=jax.Shape...]
    pmax x1 -> x0, blocking collectives: 26.9 us -> none  [local_step(): global_max = lax.pmax(block_max, 'sp')]
    dot_general x1 -> x0, matrix products: 7.31 us -> none  [local_step(): jnp.dot(attn_out.astype(jnp.bfloat16), w_o, preferred_element_type=jnp.fl...]
    unnamed x10 -> x7, local copies, waits for them, and re-layouts: 1.09 us -> 5.22 us
    convert_element_type x2 -> x0, other arithmetic: 3.26 us -> none  [the longest x1 1.68 us: local_step(): attn_out.astype(jnp.bfloat16)]
    div x1 -> x0, local copies, waits for them, and re-layouts: 3.15 us -> none  [local_step(): merged[..., :head_dim] / merged[..., head_dim:]]
    broadcast_in_dim x1, local copies, waits for them, and re-layouts: 3.21 us -> 0.76 us  [finish(): w_post[None]]
  transfers between devices with their start and end apart: 2 -> 0, of which waited for: 2 -> 0; matrix products, arithmetic and copies ran while one was open for 0% -> 0% of each run, Pallas kernels for 0% -> 0%
where the time goes in v1:
time: 90.7 us; the launch traced here: 90.3 us
  Pallas kernels  37 us (41%)
  matrix products  24.1 us (27%)
  other arithmetic  21.3 us (23%)
  local copies, waits for them, and re-layouts  7.03 us (8%)
    pallas_call x1, Pallas kernels, finish(): pl.pallas_call(functools.partial(comm_kernel, heads), out_shape=jax.Shape...  37 us
    select_n x1, other arithmetic, local_step(): v_out = jnp.where(slot_hit, v_new[:, None], v_cache)  14.4 us
    dot_general x1, matrix products, local_step(): q_proj = jnp.dot(normed, w_q, preferred_element_type=jnp.float32)  5.84 us
    dot_general x1, matrix products, local_step(): jnp.einsum('bgrt,btgd->bgrd', exp_w.astype(jnp.bfloat16), v_out, preferre...  5.79 us
    unnamed x7, local copies, waits for them, and re-layouts  5.22 us
    dot_general x1, matrix products, local_step(): jnp.einsum('bgrd,btgd->bgrt', q_rot, k_out, preferred_element_type=jnp.fl...  4.93 us
    dot_general x1, matrix products, local_step(): jnp.dot(normed, w_v, preferred_element_type=jnp.float32)  4.01 us
    dot_general x1, matrix products, local_step(): k_proj = jnp.dot(normed, w_k, preferred_element_type=jnp.float32)  3.49 us

profile of v1, /device:TPU:97, one launch (start us, length us, event | category | flops | bytes accessed | tf_op | source)
XLA Modules:
  0.0 90.3 jit_solution(8420964146192084717)
XLA Ops:
  0.6 0.7 convert_element_type.34
  1.3 1.7 %fusion.4 = f32[128]{0:T(128)S(1)} fusion(bf16[128,5376]{1,0:T(8,128)(2,1)} %x_hbm.1), kind=kLoop, calls=%fused_computation.8 | loop fusion | flops 2064256 | bytes 1376768 | tf_op jit(solution)/shard_map/reduce_sum | solution.py:19
  3.0 0.8 broadcast_in_dim.66.wpost_ref
  3.8 0.7 broadcast_add_fusion
  4.5 0.7 broadcast_compare_fusion.1
  5.3 0.3 multiply_cosine_fusion
  5.6 4.0 %convolution_convert_fusion = bf16[128,512]{1,0:T(8,128)(2,1)S(1)} fusion(bf16[5376,512]{1,0:T(8,128)(2,1)} %param.15, bf16[128,5376]{1,0:T(8,128)(2,1)} %x_hbm.1, f32[5376]{0:T(1024)S(1)} %broadcast_add_fusion, f32[128]{0:T(128)S(1)} %add_rsqrt_fusion), kind=kOutput, calls=%fused_computation.14 | convolution fusion | flops 707461120 | bytes 7034368 | tf_op jit(solution)/shard_map/dot_general | solution.py:344
  9.7 3.5 %fusion.27 = f32[128,512]{1,0:T(8,128)S(1)} fusion(bf16[5376,512]{1,0:T(8,128)(2,1)} %param.14, bf16[128,5376]{1,0:T(8,128)(2,1)S(1)} %copy-done, f32[5376]{0:T(1024)S(1)} %broadcast_add_fusion, f32[128]{0:T(128)S(1)} %add_rsqrt_fusion), kind=kOutput, calls=%fused_computation.38 | convolution fusion | flops 707395584 | bytes 7165440 | tf_op jit(solution)/shard_map/dot_general | solution.py:342
  13.3 0.3 subtract_convert_fusion.1
  13.6 0.2 pad_maximum_fusion.1
  13.8 5.8 %fusion.29 = f32[128,1024]{1,0:T(8,128)S(1)} fusion(bf16[5376,1024]{1,0:T(8,128)(2,1)} %param.13, bf16[128,5376]{1,0:T(8,128)(2,1)S(1)} %copy-done, f32[5376]{0:T(1024)S(1)} %broadcast_add_fusion, f32[128]{0:T(128)S(1)} %add_rsqrt_fusion), kind=kOutput, calls=%fused_computation.39 | convolution fusion | flops 1412038656 | bytes 12932608 | tf_op jit(solution)/shard_map/dot_general | solution.py:340
  19.6 0.4 reshape.211
  20.1 0.8 subtract_convert_fusion
  20.9 14.4 %broadcast_select_fusion = (bf16[128,64,4,128]{3,2,1,0:T(4,128)(2,1)}, bf16[128,64,4,128]{3,2,1,0:T(4,128)(2,1)S(1)}) fusion(bf16[128,64,4,128]{3,2,1,0:T(4,128)(2,1)} %param.19, pred[128,64]{1,0:T(8,128)(4,1)S(1)} %get-tuple-element.10, bf16[128,4,128]{2,1,0:T(4,128)(2,1)S(1)} %convert_element_type.37, bf16[128,64,4,128]{3,2,1,0:T(4,128)(2,1)} %param.18, ...), kind=kLoop, calls=%fused_computation.4 | loop fusion | flops 8388608 | bytes 33824768 | tf_op jit(solution)/shard_map/jit(_where)/select_n | solution.py:348
  35.4 4.9 %fusion.31 = (f32[128,4,2]{2,1,0:T(4,128)S(1)}, f32[128,4,2,64]{3,2,1,0:T(2,128)S(1)}) fusion(bf16[128,64,4,128]{3,2,1,0:T(4,128)(2,1)S(1)} %get-tuple-element.19, bf16[128,4,2,64]{3,2,1,0:T(2,128)(2,1)S(1)} %get-tuple-element.4, bf16[128,4,2,64]{3,2,1,0:T(2,128)(2,1)S(1)} %get-tuple-element.3, pred[128,64]{1,0:T(8,128)(4,1)S(1)} %get-tuple-element.9), kind=kOutput, calls=%fused_computation.40 | convolution fusion | flops 17562624 | bytes 8925184 | tf_op jit(solution)/shard_map/bgrd,btgd->bgrt/dot_general | solution.py:349
  40.3 0.1 copy.26
  40.4 0.1 reshape.213
  40.5 1.4 %fusion.23 = f32[128,4,2]{2,1,0:T(4,128)S(1)} fusion(f32[128,4,2,64]{3,2,1,0:T(2,128)S(1)} %get-tuple-element.14, f32[128,4,2]{2,1,0:T(4,128)S(1)} %get-tuple-element.13, pred[128,64]{1,0:T(8,128)(4,1)S(1)} %get-tuple-element.9), kind=kLoop, calls=%fused_computation.31 | loop fusion | flops 195584 | bytes 278528 | tf_op jit(solution)/shard_map/reduce_sum | solution.py:355
  41.9 5.8 %fusion = f32[128,4,2,128]{3,2,1,0:T(2,128)S(1)} fusion(bf16[128,64,4,128]{3,2,1,0:T(4,128)(2,1)} %get-tuple-element.20, f32[128,4,2,64]{3,2,1,0:T(2,128)S(1)} %get-tuple-element.14, pred[128,64]{1,0:T(8,128)(4,1)S(1)} %get-tuple-element.9, f32[128,4,2]{2,1,0:T(4,128)S(1)} %get-tuple-element.13), kind=kOutput, calls=%fused_computation | convolution fusion | flops 16973824 | bytes 9187328 | tf_op jit(solution)/shard_map/bgrt,btgd->bgrd/dot_general | solution.py:356
  47.7 0.1 copy.28
  47.8 0.1 reshape.214
  48.0 4.1 %copy-done.1 = bf16[1024,5376]{1,0:T(8,128)(2,1)S(1)} copy-done((bf16[1024,5376]{1,0:T(8,128)(2,1)S(1)}, bf16[1024,5376]{1,0:T(8,128)(2,1)}, u32[]{:S(2)}) %copy-start.1) | copy-done | bytes 11010072
  52.2 37.0 %finish.1 = bf16[128,5376]{1,0:T(8,128)(2,1)S(1)} custom-call(f32[8,144,128]{2,1,0:T(8,128)S(1)} %bitcast.15, bf16[1024,5376]{1,0:T(8,128)(2,1)S(1)} %copy-done.1, bf16[128,5376]{1,0:T(8,128)(2,1)S(1)} %copy-done, f32[1,5376]{1,0:T(1,128)S(1)} %broadcast_in_dim.66.wpost_ref), custom_call_target="tpu_custom_call" | custom-call | flops 176160768 | bytes 11010048 | tf_op jit(solution)/shard_map/finish/pallas_call | solution.py:301
  89.2 1.1 %copy.54 = bf16[128,5376]{1,0:T(8,128)(2,1)} copy(bf16[128,5376]{1,0:T(8,128)(2,1)S(1)} %finish.1) | data formatting | bytes 2752512
  (15 shorter events, 0.3 us)
Async XLA Ops:
  5.6 4.1 %copy-start = (bf16[128,5376]{1,0:T(8,128)(2,1)S(1)}, bf16[128,5376]{1,0:T(8,128)(2,1)}, u32[]{:S(2)}) copy-start(bf16[128,5376]{1,0:T(8,128)(2,1)} %x_hbm.1) | copy-start | bytes 4128772
  35.3 4.9 %copy-start.2 = (bf16[128,64,4,128]{3,2,1,0:T(4,128)(2,1)}, bf16[128,64,4,128]{3,2,1,0:T(4,128)(2,1)S(1)}, u32[]{:S(2)}) copy-start(bf16[128,64,4,128]{3,2,1,0:T(4,128)(2,1)S(1)} %get-tuple-element.19) | copy-start | bytes 25165828
  48.0 4.1 %copy-start.1 = (bf16[1024,5376]{1,0:T(8,128)(2,1)S(1)}, bf16[1024,5376]{1,0:T(8,128)(2,1)}, u32[]{:S(2)}) copy-start(bf16[1024,5376]{1,0:T(8,128)(2,1)} %wo_hbm.1) | copy-start | bytes 33030148

commit v2 on v1

--- a/solution.py
+++ b/solution.py
@@ -13,23 +13,6 @@
 NEG_FILL = -1e30
 MESH = pl.DeviceIdType.MESH
 RING = 4
-
-
-def rms_scale(tensor, gain_w):
-    mean_sq = jnp.mean(tensor * tensor, axis=-1, keepdims=True)
-    return tensor * lax.rsqrt(mean_sq + NORM_EPS) * (1.0 + gain_w)
-
-
-def rotary(tensor, positions):
-    half_dim = tensor.shape[-1] // 2
-    inv_freq = ROPE_BASE ** (-2.0 * jnp.arange(half_dim, dtype=jnp.float32) / (2 * half_dim))
-    angles = positions.astype(jnp.float32)[:, None] * inv_freq[None, :]
-    angles = angles.reshape((angles.shape[0],) + (1,) * (tensor.ndim - 2) + (half_dim,))
-    cos_tab = jnp.cos(angles)
-    sin_tab = jnp.sin(angles)
-    lo_half = tensor[..., :half_dim]
-    hi_half = tensor[..., half_dim:]
-    return jnp.concatenate([lo_half * cos_tab - hi_half * sin_tab, hi_half * cos_tab + lo_half * sin_tab], axis=-1)
 
 
 FIRST_P, FIRST_M, DIAG_A, DIAG_B = 0, 1, 2, 3
@@ -291,6 +274,172 @@
         copy.wait_send()
 
 
+def attend_kernel(kv_heads, pos_ref, x_ref, wpre_ref, cos_ref, sin_ref, wq_hbm, wk_hbm, wv_hbm, kc_hbm, vc_hbm,
+                  pack_ref, ko_hbm, vo_hbm, a_v, w_v, q_s, kn_s, vn_s, ko_ref, vo_ref, w_sem, k_sem, v_sem, ko_sem, vo_sem):
+    rows, width = x_ref.shape
+    dim = pack_ref.shape[2]
+    n_slab = pack_ref.shape[0]
+    row_block = rows // n_slab
+    heads = q_s.shape[0] // rows
+    group = heads // kv_heads
+    span = ko_ref.shape[1]
+    seq_block = span // kv_heads
+    window = kn_s.shape[0] // rows
+    chunk = w_v.shape[2]
+    first_pos = lax.axis_index('sp') * seq_block
+
+    jobs = [('k', wk_hbm, i) for i in range(wk_hbm.shape[1] // chunk)]
+    jobs += [('v', wv_hbm, i) for i in range(wv_hbm.shape[1] // chunk)]
+    jobs += [('q', wq_hbm, i) for i in range(wq_hbm.shape[1] // chunk)]
+
+    def w_copy(n):
+        _, ref, i = jobs[n]
+        return pltpu.make_async_copy(ref.at[:, pl.ds(i * chunk, chunk)], w_v.at[n], w_sem.at[n])
+
+    def slab_copies(d):
+        part = pl.ds(d * row_block, row_block)
+        return (pltpu.make_async_copy(kc_hbm.at[part], ko_ref.at[part], k_sem.at[d]),
+                pltpu.make_async_copy(vc_hbm.at[part], vo_ref.at[part], v_sem.at[d]))
+
+    def out_copies(d):
+        part = pl.ds(d * row_block, row_block)
+        return (pltpu.make_async_copy(ko_ref.at[part], ko_hbm.at[part], ko_sem.at[d]),
+                pltpu.make_async_copy(vo_ref.at[part], vo_hbm.at[part], vo_sem.at[d]))
+
+    for n in range(len(jobs)):
+        w_copy(n).start()
+
+    n_piece = 6 if width % (6 * 128) == 0 else 1
+    piece = width // n_piece
+
+    @pl.loop(0, rows // 16)
+    def _(i):
+        part = pl.ds(pl.multiple_of(i * 16, 16), 16)
+        ssq = jnp.zeros((16, 1), jnp.float32)
+        for n in range(n_piece):
+            xf = x_ref[part, pl.ds(n * piece, piece)].astype(jnp.float32)
+            ssq += jnp.sum(xf * xf, axis=1, keepdims=True)
+        scale = lax.rsqrt(ssq / width + NORM_EPS)
+        for n in range(n_piece):
+            cols = pl.ds(n * piece, piece)
+            xf = x_ref[part, cols].astype(jnp.float32)
+            a_v[part, cols] = (xf * scale * (1.0 + wpre_ref[:, cols])).astype(a_v.dtype)
+
+    half = dim // 2
+    cos_all = jnp.concatenate([cos_ref[...], cos_ref[...]], axis=1)
+    sin_all = jnp.concatenate([-sin_ref[...], sin_ref[...]], axis=1)
+    slabs_started = 0
+    for n, (kind, _, i) in enumerate(jobs):
+        w_copy(n).wait()
+        upto = n_slab * (n + 1) // len(jobs)
+        for d in range(slabs_started, upto):
+            for copy in slab_copies(d):
+                copy.start()
+        slabs_started = upto
+        prod = jnp.dot(a_v[...], w_v[n], preferred_element_type=jnp.float32)
+        for h in range(chunk // dim):
+            val = prod[:, h * dim:(h + 1) * dim]
+            if kind != 'v':
+                val = val * cos_all + pltpu.roll(val, half, 1) * sin_all
+            head = i * (chunk // dim) + h
+            if kind == 'q':
+                q_s[pl.ds(head, rows, stride=heads), :] = val
+            else:
+                for r in range(window // kv_heads):
+                    (kn_s if kind == 'k' else vn_s)[pl.ds(r * kv_heads + head, rows, stride=window), :] = val
+
+    col = lax.broadcasted_iota(jnp.int32, (heads, span), 1)
+    row = lax.broadcasted_iota(jnp.int32, (heads, span), 0)
+    same_head = col % kv_heads == row // group
+    lane = lax.broadcasted_iota(jnp.int32, (heads, dim), 1)
+    win_time = lax.broadcasted_iota(jnp.int32, (window, dim), 0) // kv_heads
+    per_window = window // kv_heads
+
+    @pl.loop(0, n_slab)
+    def _(d):
+        for copy in slab_copies(d):
+            copy.wait()
+        last = []
+        for j in range(row_block):
+            b = d * row_block + j
+            here = pos_ref[b] - first_pos
+            last.append(here)
+            slot = jnp.clip(here, 0, seq_block - 1)
+            at = pl.ds(pl.multiple_of(slot // per_window * window, window), window)
+            hit = win_time == jnp.where(here == slot, slot % per_window, -1)
+            new = pl.ds(pl.multiple_of(b * window, window), window)
+            ko_ref[b, at, :] = jnp.where(hit, kn_s[new, :], ko_ref[b, at, :].astype(jnp.float32)).astype(ko_ref.dtype)
+            vo_ref[b, at, :] = jnp.where(hit, vn_s[new, :], vo_ref[b, at, :].astype(jnp.float32)).astype(vo_ref.dtype)
+        for copy in out_copies(d):
+            copy.start()
+        scores = []
+        for j in range(row_block):
+            b = d * row_block + j
+            q_b = q_s[pl.ds(pl.multiple_of(b * heads, heads), heads), :].astype(jnp.bfloat16)
+            scores.append(lax.dot_general(q_b, ko_ref[b], (((1,), (1,)), ((), ())), preferred_element_type=jnp.float32))
+        tops = jnp.zeros((heads, dim), jnp.float32)
+        sums = jnp.zeros((heads, dim), jnp.float32)
+        weights = []
+        for j in range(row_block):
+            valid = same_head & (col < (last[j] + 1) * kv_heads)
+            capped = jnp.where(valid, SOFT_CAP * jnp.tanh(scores[j] * (dim ** -0.5 / SOFT_CAP)), NEG_FILL)
+            top = jnp.max(capped, axis=1, keepdims=True)
+            exp_w = jnp.where(valid, jnp.exp(capped - top), 0.0)
+            tops = jnp.where(lane == j, top, tops)
+            sums = jnp.where(lane == j, jnp.sum(exp_w, axis=1, keepdims=True), sums)
+            weights.append(exp_w.astype(jnp.bfloat16))
+        slab = d % 2 * (n_slab // 2) + d // 2
+        for j in range(row_block):
+            b = d * row_block + j
+            pack_ref[slab, pl.ds(j * heads, heads), :] = jnp.dot(weights[j], vo_ref[b], preferred_element_type=jnp.float32)
+        pack_ref[slab, pl.ds(row_block * heads, heads), :] = tops
+        pack_ref[slab, pl.ds((row_block + 1) * heads, heads), :] = sums
+
+    for d in range(n_slab):
+        for copy in out_copies(d):
+            copy.wait()
+
+
+def gain_row(gain_w):
+    return jnp.pad(gain_w, (0, -gain_w.shape[0] % 1024 + 1024))[None]
+
+
+def attend(x_in, cur_pos, w_pre, w_q, w_k, w_v, k_cache, v_cache, n_sp):
+    rows, seq_block, kv_heads, dim = k_cache.shape
+    width = x_in.shape[1]
+    heads = w_q.shape[1] // dim
+    chunk = 2 * dim
+    window = 16
+    n_jobs = (w_q.shape[1] + w_k.shape[1] + w_v.shape[1]) // chunk
+    inv_freq = ROPE_BASE ** (-2.0 * jnp.arange(dim // 2, dtype=jnp.float32) / dim)
+    angles = cur_pos.astype(jnp.float32)[:, None] * inv_freq[None, :]
+    flat = (rows, seq_block * kv_heads, dim)
+    sems = pltpu.SemaphoreType.DMA
+    vmem = pl.BlockSpec(memory_space=pltpu.VMEM)
+    hbm = pl.BlockSpec(memory_space=pltpu.HBM)
+    pack, k_out, v_out = pl.pallas_call(
+        functools.partial(attend_kernel, kv_heads),
+        out_shape=(jax.ShapeDtypeStruct((n_sp, rows // n_sp * heads + 2 * heads, dim), jnp.float32),
+                   jax.ShapeDtypeStruct(flat, k_cache.dtype), jax.ShapeDtypeStruct(flat, v_cache.dtype)),
+        in_specs=[pl.BlockSpec(memory_space=pltpu.SMEM), vmem, vmem, vmem, vmem, hbm, hbm, hbm, hbm, hbm],
+        out_specs=(vmem, hbm, hbm),
+        scratch_shapes=[
+            pltpu.VMEM((rows, width), jnp.bfloat16),
+            pltpu.VMEM((n_jobs, width, chunk), w_q.dtype),
+            pltpu.VMEM(((rows + 1) * heads, dim), jnp.float32),
+            pltpu.VMEM(((rows + 1) * window, dim), jnp.float32),
+            pltpu.VMEM(((rows + 1) * window, dim), jnp.float32),
+            pltpu.VMEM(flat, k_cache.dtype),
+            pltpu.VMEM(flat, v_cache.dtype),
+            sems((n_jobs,)), sems((n_sp,)), sems((n_sp,)), sems((n_sp,)), sems((n_sp,)),
+        ],
+        compiler_params=pltpu.CompilerParams(vmem_limit_bytes=48 * 2**20),
+        cost_estimate=pl.CostEstimate(flops=2 * rows * w_q.size * 2, bytes_accessed=w_q.size * 4 + k_cache.size * 4, transcendentals=0),
+        name='attend',
+    )(cur_pos, x_in, gain_row(w_pre), jnp.cos(angles), jnp.sin(angles), w_q, w_k, w_v, k_cache.reshape(flat), v_cache.reshape(flat))
+    return pack, k_out.reshape(k_cache.shape), v_out.reshape(v_cache.shape)
+
+
 def finish(o_pack, w_o, x_in, w_post, heads):
     rows, width = x_in.shape
     _, slab_rows, dim = o_pack.shape
@@ -301,7 +450,7 @@
     return pl.pallas_call(
         functools.partial(comm_kernel, heads),
         out_shape=jax.ShapeDtypeStruct((rows, width), x_in.dtype),
-        in_specs=[vmem, pl.BlockSpec(memory_space=pl.ANY), pl.BlockSpec(memory_space=pl.ANY), vmem],
+        in_specs=[vmem, pl.BlockSpec(memory_space=pltpu.HBM), pl.BlockSpec(memory_space=pltpu.HBM), vmem],
         out_specs=vmem,
         scratch_shapes=[
             pltpu.VMEM(w_o.shape, w_o.dtype),
@@ -309,7 +458,7 @@
             pltpu.VMEM((RING, slab_rows, dim), jnp.float32),
             pltpu.VMEM((RING, slab_rows, dim), jnp.float32),
             pltpu.VMEM((RING - 1, slab_rows, dim), jnp.float32),
-            pltpu.VMEM((row_block * heads, dim), jnp.float32),
+            pltpu.VMEM(((row_block + 1) * heads, dim), jnp.float32),
             pltpu.VMEM((RING, row_block // RING, width), jnp.float32),
             pltpu.VMEM((RING - 1, row_block // RING, width), jnp.float32),
             pltpu.VMEM((2 * RING * RING, row_block // RING, width), jnp.float32),
@@ -320,10 +469,10 @@
             sems((N_GATHER,)), sems((N_GATHER,)),
             sems((RING * RING,)), sems((RING * RING,)),
         ],
-        compiler_params=pltpu.CompilerParams(collective_id=0, has_side_effects=True, vmem_limit_bytes=40 * 2**20),
+        compiler_params=pltpu.CompilerParams(collective_id=0, has_side_effects=True, vmem_limit_bytes=22 * 2**20),
         cost_estimate=pl.CostEstimate(flops=2 * rows * w_o.size // 8, bytes_accessed=w_o.size * 2, transcendentals=0),
         name='finish',
-    )(o_pack, w_o, x_in, w_post[None])
+    )(o_pack, pltpu.with_memory_space_constraint(w_o, pltpu.HBM), x_in, gain_row(w_post))
 
 
 def solution(mesh):
@@ -332,37 +481,8 @@
     assert n_sp == 2 * RING and mesh.shape['tp'] == RING
 
     def local_step(x_in, cur_pos, w_pre, w_q, w_k, w_v, w_o, w_post, k_cache, v_cache):
-        row_count, seq_block, kv_local, head_dim = k_cache.shape
-        heads_local = w_q.shape[1] // head_dim
-        group_size = heads_local // kv_local
-        sp_index = lax.axis_index('sp')
-        normed = rms_scale(x_in.astype(jnp.float32), w_pre).astype(jnp.bfloat16)
-        q_proj = jnp.dot(normed, w_q, preferred_element_type=jnp.float32)
-        q_rot = rotary(q_proj.reshape(row_count, kv_local, group_size, head_dim), cur_pos).astype(jnp.bfloat16)
-        k_proj = jnp.dot(normed, w_k, preferred_element_type=jnp.float32)
-        k_new = rotary(k_proj.reshape(row_count, kv_local, head_dim), cur_pos).astype(jnp.bfloat16)
-        v_new = jnp.dot(normed, w_v, preferred_element_type=jnp.float32).reshape(row_count, kv_local, head_dim).astype(jnp.bfloat16)
-        block_pos = sp_index * seq_block + jnp.arange(seq_block)
-        slot_hit = (block_pos[None, :] == cur_pos[:, None])[:, :, None, None]
-        k_out = jnp.where(slot_hit, k_new[:, None], k_cache)
-        v_out = jnp.where(slot_hit, v_new[:, None], v_cache)
-        raw_score = jnp.einsum('bgrd,btgd->bgrt', q_rot, k_out, preferred_element_type=jnp.float32)
-        capped = SOFT_CAP * jnp.tanh(raw_score * (head_dim ** -0.5 / SOFT_CAP))
-        is_valid = (block_pos[None, :] <= cur_pos[:, None])[:, None, None, :]
-        capped = jnp.where(is_valid, capped, NEG_FILL)
-        block_max = jnp.max(capped, axis=-1)
-        exp_w = jnp.where(is_valid, jnp.exp(capped - block_max[..., None]), 0.0)
-        block_sum = jnp.sum(exp_w, axis=-1)
-        block_out = jnp.einsum('bgrt,btgd->bgrd', exp_w.astype(jnp.bfloat16), v_out, preferred_element_type=jnp.float32)
-
-        row_block = row_count // n_sp
-
-        def stat_tile(t):
-            t = t.reshape(n_sp, row_block, heads_local).transpose(0, 2, 1)
-            return jnp.pad(t, ((0, 0), (0, 0), (0, head_dim - row_block)))
-
-        slabs = jnp.concatenate([block_out.reshape(n_sp, row_block * heads_local, head_dim), stat_tile(block_max), stat_tile(block_sum)], axis=1)
-        slabs = slabs.reshape(RING, 2, *slabs.shape[1:]).transpose(1, 0, 2, 3).reshape(slabs.shape)
+        heads_local = w_q.shape[1] // k_cache.shape[3]
+        slabs, k_out, v_out = attend(x_in, cur_pos, w_pre, w_q, w_k, w_v, k_cache, v_cache, n_sp)
         x_out = finish(slabs, w_o, x_in, w_post, heads_local)
         return x_out, k_out, v_out
 

time: 90.7 us -> 61.3 us (0.68)
  matrix products: 24.1 us -> 0 us
  other arithmetic: 21.3 us -> 0.97 us
  Pallas kernels: 37 us -> 54.8 us
  local copies, waits for them, and re-layouts: 7.03 us -> 4.56 us
    dot_general x5 -> x0, matrix products: 24.1 us -> none  [the longest x1 5.84 us: local_step(): q_proj = jnp.dot(normed, w_q, preferred_element_type=jnp.float32)]
    pallas_call x0 -> x1, Pallas kernels: none -> 17.9 us  [attend(): pl.pallas_call(functools.partial(attend_kernel, kv_heads), out_shape=(jax...]
    select_n x1 -> x0, other arithmetic: 14.4 us -> none  [local_step(): v_out = jnp.where(slot_hit, v_new[:, None], v_cache)]
    reduce_sum x2 -> x0, other arithmetic: 3.06 us -> none  [the longest x1 1.68 us: rms_scale(): mean_sq = jnp.mean(tensor * tensor, axis=-1, keepdims=True)]
    unnamed x7 -> x5, local copies, waits for them, and re-layouts: 5.22 us -> 3.07 us
    pad x2, local copies, waits for them, and re-layouts: 0.04 us -> 1.49 us  [gain_row(): return jnp.pad(gain_w, (0, -gain_w.shape[0] % 1024 + 1024))[None]]
    another operation x2 -> x0, other arithmetic: 1.14 us -> none
where the time goes in v2:
time: 61.3 us; the launch traced here: 61 us
  Pallas kernels  54.8 us (89%)
  local copies, waits for them, and re-layouts  4.56 us (7%)
  other arithmetic  0.97 us (2%)
  between operations  0.66 us (1%)
    pallas_call x1, Pallas kernels, finish(): pl.pallas_call(functools.partial(comm_kernel, heads), out_shape=jax.Shape...  37 us
    pallas_call x1, Pallas kernels, attend(): pl.pallas_call(functools.partial(attend_kernel, kv_heads), out_shape=(jax...  17.9 us
    unnamed x5, local copies, waits for them, and re-layouts  3.07 us
    pad x2, local copies, waits for them, and re-layouts, gain_row(): return jnp.pad(gain_w, (0, -gain_w.shape[0] % 1024 + 1024))[None]  1.49 us

profile of v2, /device:TPU:97, one launch (start us, length us, event | category | flops | bytes accessed | tf_op | source)
XLA Modules:
  0.0 61.0 jit_solution(10301738505556063345)
XLA Ops:
  0.6 0.7 %convert_element_type.6 = f32[128]{0:T(128)S(1)} convert(s32[128]{0:T(128)} %pos_ref.1) | non-fusion elementwise | flops 128 | bytes 1024 | tf_op jit(solution)/shard_map/convert_element_type | solution.py:415
  1.3 0.7 %pad.7 = f32[7168]{0:T(1024)S(1)} pad(f32[5376]{0:T(1024)} %param.12, f32[]{:T(128)} %constant.3.clone.1), padding=0_1792 | pad | bytes 50180 | tf_op jit(solution)/shard_map/jit(_pad)/pad | solution.py:404
  2.0 0.7 %pad.8 = f32[7168]{0:T(1024)S(1)} pad(f32[5376]{0:T(1024)} %param.17, f32[]{:T(128)} %constant.3.clone.1), padding=0_1792 | pad | bytes 50180 | tf_op jit(solution)/shard_map/jit(_pad)/pad | solution.py:404
  2.8 0.3 multiply_sine_fusion
  3.1 0.0 copy-start
  3.1 1.3 %copy-done = bf16[128,5376]{1,0:T(8,128)(2,1)S(1)} copy-done((bf16[128,5376]{1,0:T(8,128)(2,1)S(1)}, bf16[128,5376]{1,0:T(8,128)(2,1)}, u32[]{:S(2)}) %copy-start) | copy-done | bytes 1376280
  4.4 0.0 copy-start.1
  4.4 0.7 %copy-done.1 = s32[128]{0:T(128)S(1)} copy-done((s32[128]{0:T(128)S(1)}, s32[128]{0:T(128)}, u32[]{:S(2)}) %copy-start.1) | copy-done | bytes 536
  5.1 17.9 %attend.1 = (f32[8,144,128]{2,1,0:T(8,128)S(1)}, bf16[128,256,128]{2,1,0:T(8,128)(2,1)}, bf16[128,256,128]{2,1,0:T(8,128)(2,1)}) custom-call(s32[128]{0:T(128)S(1)} %copy-done.1, bf16[128,5376]{1,0:T(8,128)(2,1)S(1)} %copy-done, f32[1,7168]{1,0:T(1,128)S(1)} %bitcast.7, f32[128,64]{1,0:T(8,128)S(1)} %get-tuple-element.10.cos_ref, ...), custom_call_target="tpu_custom_call" | custom-call | flops 2818572288 | bytes 38797312 | tf_op jit(solution)/shard_map/attend/pallas_call | solution.py:420
  23.0 37.0 %finish.1 = bf16[128,5376]{1,0:T(8,128)(2,1)S(1)} custom-call(f32[8,144,128]{2,1,0:T(8,128)S(1)} %get-tuple-element.6.o_ref, bf16[1024,5376]{1,0:T(8,128)(2,1)} %wo_hbm.1, bf16[128,5376]{1,0:T(8,128)(2,1)S(1)} %copy-done, f32[1,7168]{1,0:T(1,128)S(1)} %bitcast.6), custom_call_target="tpu_custom_call" | custom-call | flops 176160768 | bytes 11010048 | tf_op jit(solution)/shard_map/finish/pallas_call | solution.py:450
  59.9 1.1 %copy.14 = bf16[128,5376]{1,0:T(8,128)(2,1)} copy(bf16[128,5376]{1,0:T(8,128)(2,1)S(1)} %finish.1) | data formatting | bytes 2752512
  (1 shorter events, 0.0 us)
Async XLA Ops:
  3.1 1.3 %copy-start = (bf16[128,5376]{1,0:T(8,128)(2,1)S(1)}, bf16[128,5376]{1,0:T(8,128)(2,1)}, u32[]{:S(2)}) copy-start(bf16[128,5376]{1,0:T(8,128)(2,1)} %x_hbm.1) | copy-start | bytes 4128772
  4.4 0.7 %copy-start.1 = (s32[128]{0:T(128)S(1)}, s32[128]{0:T(128)}, u32[]{:S(2)}) copy-start(s32[128]{0:T(128)} %pos_ref.1) | copy-start | bytes 1540

commit v3 on v2

--- a/solution.py
+++ b/solution.py
@@ -15,15 +15,11 @@
 RING = 4
 
 
-FIRST_P, FIRST_M, DIAG_A, DIAG_B = 0, 1, 2, 3
-UNITS = ('own', 'prev', 'next', 'diag_a', 'diag_b')
-SECOND = {(u, d): 4 + 2 * i + j for i, u in enumerate(UNITS) for j, d in enumerate((1, -1))}
-FORWARD = {u: 14 + i for i, u in enumerate(('own_a', 'own_b', 'prev', 'next', 'diag_a', 'diag_b'))}
-N_GATHER = 20
-
-
-def comm_kernel(heads, o_ref, wo_hbm, x_hbm, wpost_ref, out_ref,
-                wo_v, x_v, pair_r, comb, sp_r, scr, part, tp_r, gath,
+N_GATHER = 30
+
+
+def comm_kernel(heads, o_ref, wo_hbm, x_hbm, wpost_hbm, out_ref,
+                wo_v, x_v, wpost_ref, pair_r, comb, sp_r, scr, part, tp_r, gath,
                 wo_sem, x_sem, pair_ss, pair_rs, sp_ss, sp_rs, tp_ss, tp_rs, ag_ss, ag_rs, dd_ss, dd_rs):
     y = lax.axis_index('tp')
     s = lax.axis_index('sp')
@@ -52,8 +48,10 @@
         rows = pl.ds(i * wo_rows, wo_rows)
         wo_copies.append(pltpu.make_async_copy(wo_hbm.at[rows], wo_v.at[rows], wo_sem.at[i]))
         wo_copies[-1].start()
-    x_copy = pltpu.make_async_copy(x_hbm.at[pl.ds(pl.multiple_of(s * row_block, row_block), row_block)], x_v, x_sem)
+    x_copy = pltpu.make_async_copy(x_hbm.at[pl.ds(pl.multiple_of(s * row_block, row_block), row_block)], x_v, x_sem.at[0])
     x_copy.start()
+    gain_copy = pltpu.make_async_copy(wpost_hbm, wpost_ref, x_sem.at[1])
+    gain_copy.start()
 
     pl.semaphore_wait(barrier, 2 * RING - 1)
 
@@ -129,6 +127,7 @@
             copy.start()
             tp_copies.append(copy)
     x_copy.wait()
+    gain_copy.wait()
     for copy in tp_copies:
         copy.wait_recv()
     ssq = jnp.zeros((sub, 1), jnp.float32)
@@ -147,35 +146,36 @@
     def place(da, db):
         return c * RING * RING + ((a + da) % RING) * RING + (b + db) % RING
 
+    per = cols // dim
     for n in range(n_chunk):
-        span = pl.ds(n * cols, cols)
-        x16 = x_v[:, span].astype(jnp.float32)
-        x4 = x16[0:sub]
-        for t in range(1, RING):
-            x4 = jnp.where(y == t, x16[t * sub:(t + 1) * sub], x4)
-        gath[place(0, 0), :, span] = x4 + u_all[n] * scale * (1.0 + wpost_ref[:, span])
+        for i in range(per):
+            span = pl.ds(n * cols + i * dim, dim)
+            x16 = x_v[:, span].astype(jnp.float32)
+            x4 = x16[0:sub]
+            for t in range(1, RING):
+                x4 = jnp.where(y == t, x16[t * sub:(t + 1) * sub], x4)
+            gain = 1.0 + wpost_ref[n * per + i:n * per + i + 1, :]
+            gath[place(0, 0), :, span] = x4 + u_all[n][:, i * dim:(i + 1) * dim] * scale * gain
 
     def device(da, db):
         return chip(da * (1 - c) + db * c, db * (1 - c) + da * c)
 
     half = width // 2
-    parts = {'': pl.ds(0, width), 'a': pl.ds(0, half), 'b': pl.ds(half, half)}
-
-    def message(src, part_key, to, number):
-        ref = gath.at[place(*src), :, parts[part_key]]
+    sent = []
+
+    def message(src, h, to, number):
+        ref = gath.at[place(*src), :, pl.ds(h * half, half)]
         return pltpu.make_async_remote_copy(
             src_ref=ref, dst_ref=ref, send_sem=ag_ss.at[number], recv_sem=ag_rs.at[number],
             device_id=device(*to), device_id_type=MESH)
-
-    sent = []
 
     def send(*args):
         copy = message(*args)
         copy.start()
         sent.append(copy)
 
-    def wait(src, part_key, number):
-        message(src, part_key, (0, 0), number).wait_recv()
+    def wait(src, h, number):
+        message(src, h, (0, 0), number).wait_recv()
 
     def to_pair(da, db):
         ref = gath.at[place(da, db)]
@@ -186,79 +186,77 @@
         copy.start()
         sent.append(copy)
 
-    unit = {'own': (0, ''), 'prev': (-1, ''), 'next': (1, ''), 'diag_a': (2, 'a'), 'diag_b': (2, 'b')}
-
-    def second(name):
-        da, key = unit[name]
-        for d in (1, -1):
-            send((da, 0), key, (0, d), SECOND[name, d])
-
-    def got_second(name, d):
-        da, key = unit[name]
-        wait((da, -d), key, SECOND[name, d])
-
-    def forward(da, d, key, name):
-        send((da, -d), key, (0, d), FORWARD[name])
-
-    send((0, 0), '', (1, 0), FIRST_P)
-    send((0, 0), '', (-1, 0), FIRST_M)
-    second('own')
+    sign = (1, -1)
+
+    def first(h, d):
+        send((0, 0), h, (d, 0), first_no[h, d])
+
+    def second(da, h):
+        for d in sign:
+            send((da, 0), h, (0, d), second_no[da % RING, h, d])
+
+    def got_second(da, h):
+        for d in (sign[h], -sign[h]):
+            wait((da, -d), h, second_no[da % RING, h, d])
+            if d == sign[h]:
+                send((da, -d), h, (0, d), forward_no[da % RING, h])
+
+    def pairs(da):
+        to_pair(da, -1)
+        to_pair(da, 1)
+
+    numbers = iter(range(N_GATHER))
+    first_no = {(h, d): next(numbers) for h in (0, 1) for d in sign}
+    diag_no = {h: next(numbers) for h in (0, 1)}
+    second_no = {(k, h, d): next(numbers) for k in range(RING) for h in (0, 1) for d in sign}
+    forward_no = {(k, h): next(numbers) for k in range(RING) for h in (0, 1)}
+
+    for h in (0, 1):
+        first(h, 1)
+        first(h, -1)
+        second(0, h)
     to_pair(0, 0)
-    wait((-1, 0), '', FIRST_P)
-    send((-1, 0), 'a', (1, 0), DIAG_A)
-    second('prev')
+    for h in (0, 1):
+        for d in (sign[h], -sign[h]):
+            wait((-d, 0), h, first_no[h, d])
+            if d == sign[h]:
+                send((-d, 0), h, (d, 0), diag_no[h])
+            second(-d, h)
     to_pair(-1, 0)
-    wait((1, 0), '', FIRST_M)
-    send((1, 0), 'b', (-1, 0), DIAG_B)
-    second('next')
     to_pair(1, 0)
-    got_second('own', 1)
-    forward(0, 1, 'a', 'own_a')
-    to_pair(0, -1)
-    got_second('own', -1)
-    forward(0, -1, 'b', 'own_b')
-    to_pair(0, 1)
-    wait((2, 0), 'a', DIAG_A)
-    second('diag_a')
-    wait((2, 0), 'b', DIAG_B)
-    second('diag_b')
+    for h in (0, 1):
+        got_second(0, h)
+    pairs(0)
+    for h in (0, 1):
+        wait((2, 0), h, diag_no[h])
+        second(2, h)
     to_pair(2, 0)
-    got_second('prev', 1)
-    forward(-1, 1, '', 'prev')
-    to_pair(-1, -1)
-    got_second('next', -1)
-    forward(1, -1, '', 'next')
-    to_pair(1, 1)
-    got_second('prev', -1)
-    to_pair(-1, 1)
-    got_second('next', 1)
-    to_pair(1, -1)
-    wait((0, 2), 'a', FORWARD['own_a'])
-    wait((0, 2), 'b', FORWARD['own_b'])
+    for h in (0, 1):
+        got_second(-1, h)
+        got_second(1, h)
+    pairs(-1)
+    pairs(1)
+    for h in (0, 1):
+        wait((0, 2), h, forward_no[0, h])
     to_pair(0, 2)
-    got_second('diag_a', 1)
-    forward(2, 1, 'a', 'diag_a')
-    got_second('diag_b', -1)
-    forward(2, -1, 'b', 'diag_b')
-    got_second('diag_b', 1)
-    to_pair(2, -1)
-    got_second('diag_a', -1)
-    to_pair(2, 1)
-    wait((-1, 2), '', FORWARD['prev'])
-    to_pair(-1, 2)
-    wait((1, 2), '', FORWARD['next'])
-    to_pair(1, 2)
-    wait((2, 2), 'a', FORWARD['diag_a'])
-    wait((2, 2), 'b', FORWARD['diag_b'])
-    to_pair(2, 2)
-
-    a2, b2 = b, a
+    for h in (0, 1):
+        got_second(2, h)
+    pairs(2)
+    for k in (-1, 1, 2):
+        for h in (0, 1):
+            wait((k, 2), h, forward_no[k % RING, h])
+        to_pair(k, 2)
+
+    def from_pair(da, db):
+        ref = gath.at[(1 - c) * RING * RING + ((b + da) % RING) * RING + (a + db) % RING]
+        number = da % RING * RING + db % RING
+        pltpu.make_async_remote_copy(
+            src_ref=ref, dst_ref=ref, send_sem=dd_ss.at[number], recv_sem=dd_rs.at[number],
+            device_id=partner, device_id_type=MESH).wait_recv()
+
     for da in range(RING):
         for db in range(RING):
-            ref = gath.at[(1 - c) * RING * RING + ((a2 + da) % RING) * RING + (b2 + db) % RING]
-            pltpu.make_async_remote_copy(
-                src_ref=ref, dst_ref=ref, send_sem=dd_ss.at[da * RING + db], recv_sem=dd_rs.at[da * RING + db],
-                device_id=partner, device_id_type=MESH).wait_recv()
+            from_pair(da, db)
 
     for cx in range(RING):
         for cc in range(2):
@@ -274,8 +272,8 @@
         copy.wait_send()
 
 
-def attend_kernel(kv_heads, pos_ref, x_ref, wpre_ref, cos_ref, sin_ref, wq_hbm, wk_hbm, wv_hbm, kc_hbm, vc_hbm,
-                  pack_ref, ko_hbm, vo_hbm, a_v, w_v, q_s, kn_s, vn_s, ko_ref, vo_ref, w_sem, k_sem, v_sem, ko_sem, vo_sem):
+def attend_kernel(kv_heads, freq_ref, pos_hbm, x_hbm, wpre_hbm, wq_hbm, wk_hbm, wv_hbm, kc_hbm, vc_hbm,
+                  pack_ref, ko_hbm, vo_hbm, pos_ref, posv_ref, x_ref, wpre_ref, a_v, w_v, q_s, kn_s, vn_s, ko_ref, vo_ref, in_sem, w_sem, k_sem, v_sem, ko_sem, vo_sem):
     rows, width = x_ref.shape
     dim = pack_ref.shape[2]
     n_slab = pack_ref.shape[0]
@@ -306,28 +304,34 @@
         return (pltpu.make_async_copy(ko_ref.at[part], ko_hbm.at[part], ko_sem.at[d]),
                 pltpu.make_async_copy(vo_ref.at[part], vo_hbm.at[part], vo_sem.at[d]))
 
+    small = [pltpu.make_async_copy(a, b, in_sem.at[i]) for i, (a, b) in enumerate(
+        ((x_hbm, x_ref), (wpre_hbm, wpre_ref), (pos_hbm, pos_ref), (pos_hbm, posv_ref)))]
+    for copy in small:
+        copy.start()
     for n in range(len(jobs)):
         w_copy(n).start()
-
-    n_piece = 6 if width % (6 * 128) == 0 else 1
-    piece = width // n_piece
+    for copy in small:
+        copy.wait()
 
     @pl.loop(0, rows // 16)
     def _(i):
         part = pl.ds(pl.multiple_of(i * 16, 16), 16)
-        ssq = jnp.zeros((16, 1), jnp.float32)
-        for n in range(n_piece):
-            xf = x_ref[part, pl.ds(n * piece, piece)].astype(jnp.float32)
-            ssq += jnp.sum(xf * xf, axis=1, keepdims=True)
-        scale = lax.rsqrt(ssq / width + NORM_EPS)
-        for n in range(n_piece):
-            cols = pl.ds(n * piece, piece)
+        squares = jnp.zeros((16, dim), jnp.float32)
+        for n in range(width // dim):
+            xf = x_ref[part, pl.ds(n * dim, dim)].astype(jnp.float32)
+            squares += xf * xf
+        scale = lax.rsqrt(jnp.sum(squares, axis=1, keepdims=True) / width + NORM_EPS)
+        for n in range(width // dim):
+            cols = pl.ds(n * dim, dim)
             xf = x_ref[part, cols].astype(jnp.float32)
-            a_v[part, cols] = (xf * scale * (1.0 + wpre_ref[:, cols])).astype(a_v.dtype)
+            a_v[part, cols] = (xf * scale * (1.0 + wpre_ref[n:n + 1, :])).astype(a_v.dtype)
 
     half = dim // 2
-    cos_all = jnp.concatenate([cos_ref[...], cos_ref[...]], axis=1)
-    sin_all = jnp.concatenate([-sin_ref[...], sin_ref[...]], axis=1)
+    positions = jnp.broadcast_to(posv_ref[...].astype(jnp.float32), (dim, rows)).T
+    angles = positions * freq_ref[0:1, :]
+    cos_all = jnp.cos(angles)
+    sin_all = jnp.sin(angles)
+    sin_all = jnp.where(lax.broadcasted_iota(jnp.int32, sin_all.shape, 1) < half, -sin_all, sin_all)
     slabs_started = 0
     for n, (kind, _, i) in enumerate(jobs):
         w_copy(n).wait()
@@ -362,7 +366,7 @@
         last = []
         for j in range(row_block):
             b = d * row_block + j
-            here = pos_ref[b] - first_pos
+            here = pos_ref[0, b] - first_pos
             last.append(here)
             slot = jnp.clip(here, 0, seq_block - 1)
             at = pl.ds(pl.multiple_of(slot // per_window * window, window), window)
@@ -400,8 +404,8 @@
             copy.wait()
 
 
-def gain_row(gain_w):
-    return jnp.pad(gain_w, (0, -gain_w.shape[0] % 1024 + 1024))[None]
+def in_hbm(operand):
+    return pltpu.with_memory_space_constraint(operand, pltpu.HBM)
 
 
 def attend(x_in, cur_pos, w_pre, w_q, w_k, w_v, k_cache, v_cache, n_sp):
@@ -412,7 +416,7 @@
     window = 16
     n_jobs = (w_q.shape[1] + w_k.shape[1] + w_v.shape[1]) // chunk
     inv_freq = ROPE_BASE ** (-2.0 * jnp.arange(dim // 2, dtype=jnp.float32) / dim)
-    angles = cur_pos.astype(jnp.float32)[:, None] * inv_freq[None, :]
+    freq = jnp.broadcast_to(jnp.concatenate([inv_freq, inv_freq])[None], (8, dim))
     flat = (rows, seq_block * kv_heads, dim)
     sems = pltpu.SemaphoreType.DMA
     vmem = pl.BlockSpec(memory_space=pltpu.VMEM)
@@ -421,9 +425,13 @@
         functools.partial(attend_kernel, kv_heads),
         out_shape=(jax.ShapeDtypeStruct((n_sp, rows // n_sp * heads + 2 * heads, dim), jnp.float32),
                    jax.ShapeDtypeStruct(flat, k_cache.dtype), jax.ShapeDtypeStruct(flat, v_cache.dtype)),
-        in_specs=[pl.BlockSpec(memory_space=pltpu.SMEM), vmem, vmem, vmem, vmem, hbm, hbm, hbm, hbm, hbm],
+        in_specs=[vmem] + [hbm] * 8,
         out_specs=(vmem, hbm, hbm),
         scratch_shapes=[
+            pltpu.SMEM((1, rows), cur_pos.dtype),
+            pltpu.VMEM((1, rows), cur_pos.dtype),
+            pltpu.VMEM((rows, width), x_in.dtype),
+            pltpu.VMEM((width // dim, dim), jnp.float32),
             pltpu.VMEM((rows, width), jnp.bfloat16),
             pltpu.VMEM((n_jobs, width, chunk), w_q.dtype),
             pltpu.VMEM(((rows + 1) * heads, dim), jnp.float32),
@@ -431,12 +439,13 @@
             pltpu.VMEM(((rows + 1) * window, dim), jnp.float32),
             pltpu.VMEM(flat, k_cache.dtype),
             pltpu.VMEM(flat, v_cache.dtype),
-            sems((n_jobs,)), sems((n_sp,)), sems((n_sp,)), sems((n_sp,)), sems((n_sp,)),
+            sems((4,)), sems((n_jobs,)), sems((n_sp,)), sems((n_sp,)), sems((n_sp,)), sems((n_sp,)),
         ],
         compiler_params=pltpu.CompilerParams(vmem_limit_bytes=48 * 2**20),
         cost_estimate=pl.CostEstimate(flops=2 * rows * w_q.size * 2, bytes_accessed=w_q.size * 4 + k_cache.size * 4, transcendentals=0),
         name='attend',
-    )(cur_pos, x_in, gain_row(w_pre), jnp.cos(angles), jnp.sin(angles), w_q, w_k, w_v, k_cache.reshape(flat), v_cache.reshape(flat))
+    )(freq, in_hbm(cur_pos[None]), in_hbm(x_in), in_hbm(w_pre.reshape(-1, dim)),
+      in_hbm(w_q), in_hbm(w_k), in_hbm(w_v), in_hbm(k_cache.reshape(flat)), in_hbm(v_cache.reshape(flat)))
     return pack, k_out.reshape(k_cache.shape), v_out.reshape(v_cache.shape)
 
 
@@ -447,14 +456,16 @@
     n_chunk = 3 if width % (3 * 256) == 0 else 1
     sems = pltpu.SemaphoreType.DMA
     vmem = pl.BlockSpec(memory_space=pltpu.VMEM)
+    hbm = pl.BlockSpec(memory_space=pltpu.HBM)
     return pl.pallas_call(
         functools.partial(comm_kernel, heads),
         out_shape=jax.ShapeDtypeStruct((rows, width), x_in.dtype),
-        in_specs=[vmem, pl.BlockSpec(memory_space=pltpu.HBM), pl.BlockSpec(memory_space=pltpu.HBM), vmem],
+        in_specs=[vmem, hbm, hbm, hbm],
         out_specs=vmem,
         scratch_shapes=[
             pltpu.VMEM(w_o.shape, w_o.dtype),
             pltpu.VMEM((row_block, width), x_in.dtype),
+            pltpu.VMEM((width // dim, dim), jnp.float32),
             pltpu.VMEM((RING, slab_rows, dim), jnp.float32),
             pltpu.VMEM((RING, slab_rows, dim), jnp.float32),
             pltpu.VMEM((RING - 1, slab_rows, dim), jnp.float32),
@@ -462,7 +473,7 @@
             pltpu.VMEM((RING, row_block // RING, width), jnp.float32),
             pltpu.VMEM((RING - 1, row_block // RING, width), jnp.float32),
             pltpu.VMEM((2 * RING * RING, row_block // RING, width), jnp.float32),
-            sems((RING,)), sems(()),
+            sems((RING,)), sems((2,)),
             sems((RING,)), sems((RING,)),
             sems((RING - 1,)), sems((RING - 1,)),
             sems((n_chunk * (RING - 1),)), sems((n_chunk * (RING - 1),)),
@@ -472,7 +483,7 @@
         compiler_params=pltpu.CompilerParams(collective_id=0, has_side_effects=True, vmem_limit_bytes=22 * 2**20),
         cost_estimate=pl.CostEstimate(flops=2 * rows * w_o.size // 8, bytes_accessed=w_o.size * 2, transcendentals=0),
         name='finish',
-    )(o_pack, pltpu.with_memory_space_constraint(w_o, pltpu.HBM), x_in, gain_row(w_post))
+    )(o_pack, in_hbm(w_o), in_hbm(x_in), in_hbm(w_post.reshape(-1, dim)))
 
 
 def solution(mesh):

time: 61.3 us -> 62.1 us (1.013)
  Pallas kernels: 54.8 us -> 60.2 us
  local copies, waits for them, and re-layouts: 4.56 us -> 1.09 us
  other arithmetic: 0.97 us -> 0.09 us
    pallas_call x1, Pallas kernels: 17.9 us -> 23.3 us  [attend(): pl.pallas_call(functools.partial(attend_kernel, kv_heads), out_shape=(jax...]
    unnamed x5 -> x1, local copies, waits for them, and re-layouts: 3.07 us -> 1.08 us
    pad x2 -> x0, local copies, waits for them, and re-layouts: 1.49 us -> none  [gain_row(): return jnp.pad(gain_w, (0, -gain_w.shape[0] % 1024 + 1024))[None]]
    convert_element_type x1 -> x0, other arithmetic: 0.66 us -> none  [attend(): angles = cur_pos.astype(jnp.float32)[:, None] * inv_freq[None, :]]
where the time goes in v3:
time: 62.1 us; the launch traced here: 62 us
  Pallas kernels  60.2 us (97%)
  local copies, waits for them, and re-layouts  1.09 us (2%)
  between operations  0.65 us (1%)
    pallas_call x1, Pallas kernels, finish(): pl.pallas_call(functools.partial(comm_kernel, heads), out_shape=jax.Shape...  36.9 us
    pallas_call x1, Pallas kernels, attend(): pl.pallas_call(functools.partial(attend_kernel, kv_heads), out_shape=(jax...  23.3 us

profile of v3, /device:TPU:97, one launch (start us, length us, event | category | flops | bytes accessed | tf_op | source)
XLA Modules:
  0.0 62.0 jit_solution(1718496899880191675)
XLA Ops:
  0.6 0.1 pad_maximum_fusion
  0.7 23.3 %attend.1 = (f32[8,144,128]{2,1,0:T(8,128)S(1)}, bf16[128,256,128]{2,1,0:T(8,128)(2,1)}, bf16[128,256,128]{2,1,0:T(8,128)(2,1)}) custom-call(f32[8,128]{1,0:T(8,128)S(1)} %broadcast_in_dim.4.freq_ref, s32[1,128]{1,0:T(1,128)} %bitcast.11, bf16[128,5376]{1,0:T(8,128)(2,1)} %x_hbm.3, f32[42,128]{1,0:T(8,128)} %bitcast.9, bf16[5376,1024]{1,0:T(8,128)(2,1)} %wq_hbm.1, ...), custom_call_target="tpu_custom_call" | custom-call | flops 2818572288 | bytes 38797312 | tf_op jit(solution)/shard_map/attend/pallas_call | solution.py:424
  24.0 36.9 %finish.1 = bf16[128,5376]{1,0:T(8,128)(2,1)S(1)} custom-call(f32[8,144,128]{2,1,0:T(8,128)S(1)} %get-tuple-element.6.o_ref, bf16[1024,5376]{1,0:T(8,128)(2,1)} %wo_hbm.1, bf16[128,5376]{1,0:T(8,128)(2,1)} %x_hbm.3, f32[42,128]{1,0:T(8,128)} %bitcast.10), custom_call_target="tpu_custom_call" | custom-call | flops 176160768 | bytes 11010048 | tf_op jit(solution)/shard_map/finish/pallas_call | solution.py:460
  60.9 1.1 %copy.14 = bf16[128,5376]{1,0:T(8,128)(2,1)} copy(bf16[128,5376]{1,0:T(8,128)(2,1)S(1)} %finish.1) | data formatting | bytes 2752512
  (2 shorter events, 0.0 us)

commit v4 on v3

--- a/solution.py
+++ b/solution.py
@@ -254,17 +254,19 @@
             src_ref=ref, dst_ref=ref, send_sem=dd_ss.at[number], recv_sem=dd_rs.at[number],
             device_id=partner, device_id_type=MESH).wait_recv()
 
+    def convert(kind):
+        for cx in range(RING):
+            rows = pl.ds(pl.multiple_of((2 * cx + kind) * row_block, row_block), row_block)
+            slots = [kind * RING * RING + (1 - kind) * (cx * RING + t) + kind * (t * RING + cx) for t in range(RING)]
+            for n in range(n_chunk):
+                span = pl.ds(n * cols, cols)
+                out_ref[rows, span] = jnp.concatenate([gath[i, :, span] for i in slots], axis=0).astype(out_ref.dtype)
+
+    convert(c)
     for da in range(RING):
         for db in range(RING):
             from_pair(da, db)
-
-    for cx in range(RING):
-        for cc in range(2):
-            rows = pl.ds((2 * cx + cc) * row_block, row_block)
-            for n in range(n_chunk):
-                span = pl.ds(n * cols, cols)
-                blocks = [gath[cx * RING + t if cc == 0 else RING * RING + t * RING + cx, :, span] for t in range(RING)]
-                out_ref[rows, span] = jnp.concatenate(blocks, axis=0).astype(out_ref.dtype)
+    convert(1 - c)
 
     for copy in pair:
         copy.wait_send()
@@ -308,10 +310,11 @@
         ((x_hbm, x_ref), (wpre_hbm, wpre_ref), (pos_hbm, pos_ref), (pos_hbm, posv_ref)))]
     for copy in small:
         copy.start()
-    for n in range(len(jobs)):
-        w_copy(n).start()
+    w_copy(0).start()
     for copy in small:
         copy.wait()
+    for n in range(1, len(jobs)):
+        w_copy(n).start()
 
     @pl.loop(0, rows // 16)
     def _(i):

time: 62.1 us -> 56.7 us (0.913)
  Pallas kernels: 60.2 us -> 54.8 us
    pallas_call x1, Pallas kernels: 23.3 us -> 18 us  [attend(): pl.pallas_call(functools.partial(attend_kernel, kv_heads), out_shape=(jax...]
where the time goes in v4:
time: 56.7 us; the launch traced here: 56.6 us
  Pallas kernels  54.8 us (97%)
  local copies, waits for them, and re-layouts  1.09 us (2%)
  between operations  0.65 us (1%)
    pallas_call x1, Pallas kernels, finish(): pl.pallas_call(functools.partial(comm_kernel, heads), out_shape=jax.Shape...  36.8 us
    pallas_call x1, Pallas kernels, attend(): pl.pallas_call(functools.partial(attend_kernel, kv_heads), out_shape=(jax...  18 us

profile of v4, /device:TPU:97, one launch (start us, length us, event | category | flops | bytes accessed | tf_op | source)
XLA Modules:
  0.0 56.6 jit_solution(7067914477220707002)
XLA Ops:
  0.6 0.1 pad_maximum_fusion
  0.7 18.0 %attend.1 = (f32[8,144,128]{2,1,0:T(8,128)S(1)}, bf16[128,256,128]{2,1,0:T(8,128)(2,1)}, bf16[128,256,128]{2,1,0:T(8,128)(2,1)}) custom-call(f32[8,128]{1,0:T(8,128)S(1)} %broadcast_in_dim.4.freq_ref, s32[1,128]{1,0:T(1,128)} %bitcast.11, bf16[128,5376]{1,0:T(8,128)(2,1)} %x_hbm.3, f32[42,128]{1,0:T(8,128)} %bitcast.9, bf16[5376,1024]{1,0:T(8,128)(2,1)} %wq_hbm.1, ...), custom_call_target="tpu_custom_call" | custom-call | flops 2818572288 | bytes 38797312 | tf_op jit(solution)/shard_map/attend/pallas_call | solution.py:427
  18.7 36.8 %finish.1 = bf16[128,5376]{1,0:T(8,128)(2,1)S(1)} custom-call(f32[8,144,128]{2,1,0:T(8,128)S(1)} %get-tuple-element.6.o_ref, bf16[1024,5376]{1,0:T(8,128)(2,1)} %wo_hbm.1, bf16[128,5376]{1,0:T(8,128)(2,1)} %x_hbm.3, f32[42,128]{1,0:T(8,128)} %bitcast.10), custom_call_target="tpu_custom_call" | custom-call | flops 176160768 | bytes 11010048 | tf_op jit(solution)/shard_map/finish/pallas_call | solution.py:463
  55.5 1.1 %copy.14 = bf16[128,5376]{1,0:T(8,128)(2,1)} copy(bf16[128,5376]{1,0:T(8,128)(2,1)S(1)} %finish.1) | data formatting | bytes 2752512
  (2 shorter events, 0.0 us)

commit v5 on v4

--- a/solution.py
+++ b/solution.py
@@ -15,6 +15,7 @@
 RING = 4
 
 
+GROUPS = 2
 N_GATHER = 30
 
 
@@ -26,10 +27,10 @@
     xc = s // 2
     c = s % 2
     slab_rows, dim = comb.shape[1], comb.shape[2]
-    row_block = (slab_rows - 2 * heads) // heads
-    sub = row_block // RING
-    width = part.shape[2]
-    stat = row_block * heads
+    row_block = slab_rows // heads - 2
+    group_rows = row_block // GROUPS
+    sub = group_rows // RING
+    width = part.shape[3]
 
     def chip(dx, dy):
         return {'tp': (y + dy) % RING, 'sp': ((xc + dx) % RING) * 2 + c}
@@ -54,117 +55,128 @@
     gain_copy.start()
 
     pl.semaphore_wait(barrier, 2 * RING - 1)
+    sent = []
+
+    def rows_of(g):
+        start = (2 + g * group_rows) * heads if g else 0
+        return pl.ds(start, (2 + (g + 1) * group_rows) * heads - start)
 
     order = (2, 1, 3, 0)
-    pair = []
-    for k in order:
-        there = (xc + k) % RING
-        pair.append(pltpu.make_async_remote_copy(
-            src_ref=o_ref.at[(1 - c) * RING + there], dst_ref=pair_r.at[there],
-            send_sem=pair_ss.at[k], recv_sem=pair_rs.at[k], device_id=partner, device_id_type=MESH))
-        pair[-1].start()
-    sp_copies = {}
-    for i, k in enumerate(order):
-        there = (xc + k) % RING
-        mine = c * RING + there
-        pair[i].wait_recv()
-        m0 = o_ref[mine, pl.ds(stat, heads), :]
-        l0 = o_ref[mine, pl.ds(stat + heads, heads), :]
-        m1 = pair_r[there, pl.ds(stat, heads), :]
-        l1 = pair_r[there, pl.ds(stat + heads, heads), :]
-        top = jnp.maximum(m0, m1)
-        f0 = jnp.exp(m0 - top)
-        f1 = jnp.exp(m1 - top)
-        comb[there, pl.ds(stat, heads), :] = top
-        comb[there, pl.ds(stat + heads, heads), :] = l0 * f0 + l1 * f1
-        for j in range(row_block):
-            rows = pl.ds(j * heads, heads)
-            comb[there, rows, :] = o_ref[mine, rows, :] * f0[:, j:j + 1] + pair_r[there, rows, :] * f1[:, j:j + 1]
-        if k:
-            sp_copies[k] = pltpu.make_async_remote_copy(
-                src_ref=comb.at[there], dst_ref=sp_r.at[RING - k - 1],
-                send_sem=sp_ss.at[k - 1], recv_sem=sp_rs.at[RING - k - 1], device_id=chip(k, 0), device_id_type=MESH)
-            sp_copies[k].start()
-
-    def arrived(k):
-        return pltpu.make_async_remote_copy(
-            src_ref=comb.at[xc], dst_ref=sp_r.at[k - 1], send_sem=sp_ss.at[k - 1], recv_sem=sp_rs.at[k - 1],
-            device_id=chip(k, 0), device_id_type=MESH)
-    for k in (1, 3, 2):
-        arrived(k).wait_recv()
-    m_all = [comb[xc, pl.ds(stat, heads), :]] + [sp_r[k, pl.ds(stat, heads), :] for k in range(RING - 1)]
-    l_all = [comb[xc, pl.ds(stat + heads, heads), :]] + [sp_r[k, pl.ds(stat + heads, heads), :] for k in range(RING - 1)]
-    top = functools.reduce(jnp.maximum, m_all)
-    f_all = [jnp.exp(m - top) for m in m_all]
-    total = sum(l * f for l, f in zip(l_all, f_all))
-    lane = lax.broadcasted_iota(jnp.int32, total.shape, 1)
-    inv = 1.0 / jnp.where(lane < row_block, total, 1.0)
-    f_all = [f * inv for f in f_all]
-    for j in range(row_block):
-        rows = pl.ds(j * heads, heads)
-        acc = comb[xc, rows, :] * f_all[0][:, j:j + 1]
-        for k in range(RING - 1):
-            acc += sp_r[k, rows, :] * f_all[k + 1][:, j:j + 1]
-        scr[rows, :] = acc
-    attn = jnp.concatenate([scr[pl.ds(h, row_block, stride=heads), :].astype(jnp.bfloat16) for h in range(heads)], axis=1)
-
-    for copy in wo_copies:
-        copy.wait()
-    n_chunk = tp_ss.shape[0] // (RING - 1)
+    pair = {}
+    for g in range(GROUPS):
+        for k in order:
+            there = (xc + k) % RING
+            pair[g, k] = pltpu.make_async_remote_copy(
+                src_ref=o_ref.at[(1 - c) * RING + there, rows_of(g)], dst_ref=pair_r.at[there, rows_of(g)],
+                send_sem=pair_ss.at[g * RING + k], recv_sem=pair_rs.at[g * RING + k], device_id=partner, device_id_type=MESH)
+            pair[g, k].start()
+            sent.append(pair[g, k])
+    factors = {}
+    for g in range(GROUPS):
+        for k in order:
+            there = (xc + k) % RING
+            mine = c * RING + there
+            pair[g, k].wait_recv()
+            if g == 0:
+                m0 = o_ref[mine, pl.ds(0, heads), :]
+                l0 = o_ref[mine, pl.ds(heads, heads), :]
+                m1 = pair_r[there, pl.ds(0, heads), :]
+                l1 = pair_r[there, pl.ds(heads, heads), :]
+                top = jnp.maximum(m0, m1)
+                factors[k] = jnp.exp(m0 - top), jnp.exp(m1 - top)
+                comb[there, pl.ds(0, heads), :] = top
+                comb[there, pl.ds(heads, heads), :] = l0 * factors[k][0] + l1 * factors[k][1]
+            f0, f1 = factors[k]
+            for j in range(g * group_rows, (g + 1) * group_rows):
+                rows = pl.ds((2 + j) * heads, heads)
+                comb[there, rows, :] = o_ref[mine, rows, :] * f0[:, j:j + 1] + pair_r[there, rows, :] * f1[:, j:j + 1]
+            if k:
+                slot = g * (RING - 1) + RING - k - 1
+                copy = pltpu.make_async_remote_copy(
+                    src_ref=comb.at[there, rows_of(g)], dst_ref=sp_r.at[RING - k - 1, rows_of(g)],
+                    send_sem=sp_ss.at[g * (RING - 1) + k - 1], recv_sem=sp_rs.at[slot], device_id=chip(k, 0), device_id_type=MESH)
+                copy.start()
+                sent.append(copy)
+
+    n_chunk = tp_ss.shape[0] // (GROUPS * (RING - 1))
     cols = width // n_chunk
-    tp_copies = []
-    for n in range(n_chunk):
-        span = pl.ds(n * cols, cols)
-        prod = jnp.dot(attn, wo_v[:, span], preferred_element_type=jnp.float32)
-        for t in range(RING):
-            part[t, :, span] = prod[t * sub:(t + 1) * sub]
-        for k in (2, 1, 3):
-            to = (y + k) % RING
-            copy = pltpu.make_async_remote_copy(
-                src_ref=part.at[to, :, span], dst_ref=tp_r.at[RING - k - 1, :, span],
-                send_sem=tp_ss.at[n * (RING - 1) + k - 1], recv_sem=tp_rs.at[n * (RING - 1) + RING - k - 1],
-                device_id=chip(0, k), device_id_type=MESH)
-            copy.start()
-            tp_copies.append(copy)
+    tp_copies = {g: [] for g in range(GROUPS)}
+    f_all = None
+    for g in range(GROUPS):
+        for k in (1, 3, 2):
+            pltpu.make_async_remote_copy(
+                src_ref=comb.at[xc, rows_of(g)], dst_ref=sp_r.at[k - 1, rows_of(g)],
+                send_sem=sp_ss.at[g * (RING - 1) + k - 1], recv_sem=sp_rs.at[g * (RING - 1) + k - 1],
+                device_id=chip(k, 0), device_id_type=MESH).wait_recv()
+        if g == 0:
+            m_all = [comb[xc, pl.ds(0, heads), :]] + [sp_r[k, pl.ds(0, heads), :] for k in range(RING - 1)]
+            l_all = [comb[xc, pl.ds(heads, heads), :]] + [sp_r[k, pl.ds(heads, heads), :] for k in range(RING - 1)]
+            top = functools.reduce(jnp.maximum, m_all)
+            f_all = [jnp.exp(m - top) for m in m_all]
+            total = sum(l * f for l, f in zip(l_all, f_all))
+            lane = lax.broadcasted_iota(jnp.int32, total.shape, 1)
+            inv = 1.0 / jnp.where(lane < row_block, total, 1.0)
+            f_all = [f * inv for f in f_all]
+        for j in range(group_rows):
+            row = g * group_rows + j
+            rows = pl.ds((2 + row) * heads, heads)
+            acc = comb[xc, rows, :] * f_all[0][:, row:row + 1]
+            for k in range(RING - 1):
+                acc += sp_r[k, rows, :] * f_all[k + 1][:, row:row + 1]
+            scr[g, pl.ds(j * heads, heads), :] = acc
+        attn = jnp.concatenate([scr[g, pl.ds(h, group_rows, stride=heads), :].astype(jnp.bfloat16) for h in range(heads)], axis=1)
+        if g == 0:
+            for copy in wo_copies:
+                copy.wait()
+        for n in range(n_chunk):
+            span = pl.ds(n * cols, cols)
+            prod = jnp.dot(attn, wo_v[:, span], preferred_element_type=jnp.float32)
+            for t in range(RING):
+                part[g, t, :, span] = prod[t * sub:(t + 1) * sub]
+            for k in (2, 1, 3):
+                to = (y + k) % RING
+                number = (g * n_chunk + n) * (RING - 1)
+                copy = pltpu.make_async_remote_copy(
+                    src_ref=part.at[g, to, :, span], dst_ref=tp_r.at[g, RING - k - 1, :, span],
+                    send_sem=tp_ss.at[number + k - 1], recv_sem=tp_rs.at[number + RING - k - 1],
+                    device_id=chip(0, k), device_id_type=MESH)
+                copy.start()
+                tp_copies[g].append(copy)
+                sent.append(copy)
     x_copy.wait()
     gain_copy.wait()
-    for copy in tp_copies:
-        copy.wait_recv()
-    ssq = jnp.zeros((sub, 1), jnp.float32)
-    u_all = []
-    for n in range(n_chunk):
-        span = pl.ds(n * cols, cols)
-        u = part[y, :, span]
-        for k in range(RING - 1):
-            u += tp_r[k, :, span]
-        ssq += jnp.sum(u * u, axis=1, keepdims=True)
-        u_all.append(u)
-    scale = lax.rsqrt(ssq / width + NORM_EPS)
 
     a, b = xc * (1 - c) + y * c, y * (1 - c) + xc * c
 
     def place(da, db):
         return c * RING * RING + ((a + da) % RING) * RING + (b + db) % RING
 
-    per = cols // dim
-    for n in range(n_chunk):
-        for i in range(per):
-            span = pl.ds(n * cols + i * dim, dim)
-            x16 = x_v[:, span].astype(jnp.float32)
-            x4 = x16[0:sub]
-            for t in range(1, RING):
-                x4 = jnp.where(y == t, x16[t * sub:(t + 1) * sub], x4)
-            gain = 1.0 + wpost_ref[n * per + i:n * per + i + 1, :]
-            gath[place(0, 0), :, span] = x4 + u_all[n][:, i * dim:(i + 1) * dim] * scale * gain
-
     def device(da, db):
         return chip(da * (1 - c) + db * c, db * (1 - c) + da * c)
 
-    half = width // 2
-    sent = []
-
-    def message(src, h, to, number):
-        ref = gath.at[place(*src), :, pl.ds(h * half, half)]
+    def normalise(g):
+        for copy in tp_copies[g]:
+            copy.wait_recv()
+        squares = jnp.zeros((sub, dim), jnp.float32)
+        u_all = []
+        for n in range(width // dim):
+            span = pl.ds(n * dim, dim)
+            u = part[g, y, :, span]
+            for k in range(RING - 1):
+                u += tp_r[g, k, :, span]
+            squares += u * u
+            u_all.append(u)
+        scale = lax.rsqrt(jnp.sum(squares, axis=1, keepdims=True) / width + NORM_EPS)
+        for n in range(width // dim):
+            span = pl.ds(n * dim, dim)
+            x_group = x_v[:, span].astype(jnp.float32)[g * group_rows:(g + 1) * group_rows]
+            x_own = x_group[0:sub]
+            for t in range(1, RING):
+                x_own = jnp.where(y == t, x_group[t * sub:(t + 1) * sub], x_own)
+            gath[g, place(0, 0), :, span] = x_own + u_all[n] * scale * (1.0 + wpost_ref[n:n + 1, :])
+
+    def message(src, g, to, number):
+        ref = gath.at[g, place(*src)]
         return pltpu.make_async_remote_copy(
             src_ref=ref, dst_ref=ref, send_sem=ag_ss.at[number], recv_sem=ag_rs.at[number],
             device_id=device(*to), device_id_type=MESH)
@@ -174,12 +186,12 @@
         copy.start()
         sent.append(copy)
 
-    def wait(src, h, number):
-        message(src, h, (0, 0), number).wait_recv()
-
-    def to_pair(da, db):
-        ref = gath.at[place(da, db)]
-        number = da % RING * RING + db % RING
+    def wait(src, g, number):
+        message(src, g, (0, 0), number).wait_recv()
+
+    def to_pair(da, db, g):
+        ref = gath.at[g, place(da, db)]
+        number = (g * RING + da % RING) * RING + db % RING
         copy = pltpu.make_async_remote_copy(
             src_ref=ref, dst_ref=ref, send_sem=dd_ss.at[number], recv_sem=dd_rs.at[number],
             device_id=partner, device_id_type=MESH)
@@ -187,90 +199,102 @@
         sent.append(copy)
 
     sign = (1, -1)
-
-    def first(h, d):
-        send((0, 0), h, (d, 0), first_no[h, d])
-
-    def second(da, h):
+    numbers = iter(range(N_GATHER))
+    first_no = {(g, d): next(numbers) for g in (0, 1) for d in sign}
+    diag_no = {g: next(numbers) for g in (0, 1)}
+    second_no = {(k, g, d): next(numbers) for k in range(RING) for g in (0, 1) for d in sign}
+    forward_no = {(k, g): next(numbers) for k in range(RING) for g in (0, 1)}
+
+    def second(da, g):
         for d in sign:
-            send((da, 0), h, (0, d), second_no[da % RING, h, d])
-
-    def got_second(da, h):
-        for d in (sign[h], -sign[h]):
-            wait((da, -d), h, second_no[da % RING, h, d])
-            if d == sign[h]:
-                send((da, -d), h, (0, d), forward_no[da % RING, h])
-
-    def pairs(da):
-        to_pair(da, -1)
-        to_pair(da, 1)
-
-    numbers = iter(range(N_GATHER))
-    first_no = {(h, d): next(numbers) for h in (0, 1) for d in sign}
-    diag_no = {h: next(numbers) for h in (0, 1)}
-    second_no = {(k, h, d): next(numbers) for k in range(RING) for h in (0, 1) for d in sign}
-    forward_no = {(k, h): next(numbers) for k in range(RING) for h in (0, 1)}
-
-    for h in (0, 1):
-        first(h, 1)
-        first(h, -1)
-        second(0, h)
-    to_pair(0, 0)
-    for h in (0, 1):
-        for d in (sign[h], -sign[h]):
-            wait((-d, 0), h, first_no[h, d])
-            if d == sign[h]:
-                send((-d, 0), h, (d, 0), diag_no[h])
-            second(-d, h)
-    to_pair(-1, 0)
-    to_pair(1, 0)
-    for h in (0, 1):
-        got_second(0, h)
-    pairs(0)
-    for h in (0, 1):
-        wait((2, 0), h, diag_no[h])
-        second(2, h)
-    to_pair(2, 0)
-    for h in (0, 1):
-        got_second(-1, h)
-        got_second(1, h)
-    pairs(-1)
-    pairs(1)
-    for h in (0, 1):
-        wait((0, 2), h, forward_no[0, h])
-    to_pair(0, 2)
-    for h in (0, 1):
-        got_second(2, h)
-    pairs(2)
-    for k in (-1, 1, 2):
-        for h in (0, 1):
-            wait((k, 2), h, forward_no[k % RING, h])
-        to_pair(k, 2)
-
-    def from_pair(da, db):
-        ref = gath.at[(1 - c) * RING * RING + ((b + da) % RING) * RING + (a + db) % RING]
-        number = da % RING * RING + db % RING
-        pltpu.make_async_remote_copy(
-            src_ref=ref, dst_ref=ref, send_sem=dd_ss.at[number], recv_sem=dd_rs.at[number],
-            device_id=partner, device_id_type=MESH).wait_recv()
-
-    def convert(kind):
+            send((da, 0), g, (0, d), second_no[da % RING, g, d])
+
+    def got_second(da, g):
+        for d in (sign[g], -sign[g]):
+            wait((da, -d), g, second_no[da % RING, g, d])
+            if d == sign[g]:
+                send((da, -d), g, (0, d), forward_no[da % RING, g])
+            to_pair(da, -d, g)
+
+    def got_forward(da, g):
+        wait((da, 2), g, forward_no[da % RING, g])
+        to_pair(da, 2, g)
+
+    def step_start(g):
+        for d in (sign[g], -sign[g]):
+            send((0, 0), g, (d, 0), first_no[g, d])
+        second(0, g)
+        to_pair(0, 0, g)
+
+    def step_first(g):
+        for d in (sign[g], -sign[g]):
+            wait((-d, 0), g, first_no[g, d])
+            if d == sign[g]:
+                send((-d, 0), g, (d, 0), diag_no[g])
+            second(-d, g)
+            to_pair(-d, 0, g)
+
+    def step_own(g):
+        got_second(0, g)
+
+    def step_diag(g):
+        wait((2, 0), g, diag_no[g])
+        second(2, g)
+        to_pair(2, 0, g)
+
+    def step_sides(g):
+        got_second(-sign[g], g)
+        got_second(sign[g], g)
+
+    def step_last(g):
+        got_forward(0, g)
+        got_second(2, g)
+
+    def step_end(g):
+        for k in (-sign[g], sign[g], 2):
+            got_forward(k, g)
+
+    def convert(kind, g):
         for cx in range(RING):
-            rows = pl.ds(pl.multiple_of((2 * cx + kind) * row_block, row_block), row_block)
+            rows = pl.ds(pl.multiple_of((2 * cx + kind) * row_block + g * group_rows, group_rows), group_rows)
             slots = [kind * RING * RING + (1 - kind) * (cx * RING + t) + kind * (t * RING + cx) for t in range(RING)]
             for n in range(n_chunk):
                 span = pl.ds(n * cols, cols)
-                out_ref[rows, span] = jnp.concatenate([gath[i, :, span] for i in slots], axis=0).astype(out_ref.dtype)
-
-    convert(c)
-    for da in range(RING):
-        for db in range(RING):
-            from_pair(da, db)
-    convert(1 - c)
-
-    for copy in pair:
-        copy.wait_send()
-    for copy in list(sp_copies.values()) + tp_copies + sent:
+                out_ref[rows, span] = jnp.concatenate([gath[g, i, :, span] for i in slots], axis=0).astype(out_ref.dtype)
+
+    def from_pair(g):
+        for da in range(RING):
+            for db in range(RING):
+                ref = gath.at[g, (1 - c) * RING * RING + ((b + da) % RING) * RING + (a + db) % RING]
+                number = (g * RING + da) * RING + db
+                pltpu.make_async_remote_copy(
+                    src_ref=ref, dst_ref=ref, send_sem=dd_ss.at[number], recv_sem=dd_rs.at[number],
+                    device_id=partner, device_id_type=MESH).wait_recv()
+
+    normalise(0)
+    step_start(0)
+    normalise(1)
+    step_start(1)
+    step_first(0)
+    step_own(0)
+    step_diag(0)
+    step_first(1)
+    step_sides(0)
+    step_own(1)
+    step_diag(1)
+    step_last(0)
+    step_sides(1)
+    step_end(0)
+    step_last(1)
+    step_end(1)
+    convert(c, 0)
+    from_pair(0)
+    convert(1 - c, 0)
+    convert(c, 1)
+    from_pair(1)
+    convert(1 - c, 1)
+
+    for copy in sent:
         copy.wait_send()
 
 
@@ -398,9 +422,9 @@
         slab = d % 2 * (n_slab // 2) + d // 2
         for j in range(row_block):
             b = d * row_block + j
-            pack_ref[slab, pl.ds(j * heads, heads), :] = jnp.dot(weights[j], vo_ref[b], preferred_element_type=jnp.float32)
-        pack_ref[slab, pl.ds(row_block * heads, heads), :] = tops
-        pack_ref[slab, pl.ds((row_block + 1) * heads, heads), :] = sums
+            pack_ref[slab, pl.ds((j + 2) * heads, heads), :] = jnp.dot(weights[j], vo_ref[b], preferred_element_type=jnp.float32)
+        pack_ref[slab, pl.ds(0, heads), :] = tops
+        pack_ref[slab, pl.ds(heads, heads), :] = sums
 
     for d in range(n_slab):
         for copy in out_copies(d):
@@ -456,6 +480,7 @@
     rows, width = x_in.shape
     _, slab_rows, dim = o_pack.shape
     row_block = rows // (2 * RING)
+    sub = row_block // (GROUPS * RING)
     n_chunk = 3 if width % (3 * 256) == 0 else 1
     sems = pltpu.SemaphoreType.DMA
     vmem = pl.BlockSpec(memory_space=pltpu.VMEM)
@@ -472,16 +497,16 @@
             pltpu.VMEM((RING, slab_rows, dim), jnp.float32),
             pltpu.VMEM((RING, slab_rows, dim), jnp.float32),
             pltpu.VMEM((RING - 1, slab_rows, dim), jnp.float32),
-            pltpu.VMEM(((row_block + 1) * heads, dim), jnp.float32),
-            pltpu.VMEM((RING, row_block // RING, width), jnp.float32),
-            pltpu.VMEM((RING - 1, row_block // RING, width), jnp.float32),
-            pltpu.VMEM((2 * RING * RING, row_block // RING, width), jnp.float32),
+            pltpu.VMEM((GROUPS, (row_block // GROUPS + 1) * heads, dim), jnp.float32),
+            pltpu.VMEM((GROUPS, RING, sub, width), jnp.float32),
+            pltpu.VMEM((GROUPS, RING - 1, sub, width), jnp.float32),
+            pltpu.VMEM((GROUPS, 2 * RING * RING, sub, width), jnp.float32),
             sems((RING,)), sems((2,)),
-            sems((RING,)), sems((RING,)),
-            sems((RING - 1,)), sems((RING - 1,)),
-            sems((n_chunk * (RING - 1),)), sems((n_chunk * (RING - 1),)),
+            sems((GROUPS * RING,)), sems((GROUPS * RING,)),
+            sems((GROUPS * (RING - 1),)), sems((GROUPS * (RING - 1),)),
+            sems((GROUPS * n_chunk * (RING - 1),)), sems((GROUPS * n_chunk * (RING - 1),)),
             sems((N_GATHER,)), sems((N_GATHER,)),
-            sems((RING * RING,)), sems((RING * RING,)),
+            sems((GROUPS * RING * RING,)), sems((GROUPS * RING * RING,)),
         ],
         compiler_params=pltpu.CompilerParams(collective_id=0, has_side_effects=True, vmem_limit_bytes=22 * 2**20),
         cost_estimate=pl.CostEstimate(flops=2 * rows * w_o.size // 8, bytes_accessed=w_o.size * 2, transcendentals=0),

time: 56.7 us -> 58.1 us (1.025)
  Pallas kernels: 54.8 us -> 56.2 us
    pallas_call x1, Pallas kernels: 36.8 us -> 38.3 us  [finish(): pl.pallas_call(functools.partial(comm_kernel, heads), out_shape=jax.Shape...]
where the time goes in v5:
time: 58.1 us
  Pallas kernels  56.2 us (97%)
  local copies, waits for them, and re-layouts  1.09 us (2%)
  between operations  0.65 us (1%)
    pallas_call x1, Pallas kernels, finish(): pl.pallas_call(functools.partial(comm_kernel, heads), out_shape=jax.Shape...  38.3 us
    pallas_call x1, Pallas kernels, attend(): pl.pallas_call(functools.partial(attend_kernel, kv_heads), out_shape=(jax...  18 us

profile of v5, /device:TPU:97, one launch (start us, length us, event | category | flops | bytes accessed | tf_op | source)
XLA Modules:
  0.0 58.1 jit_solution(12319649717570097045)
XLA Ops:
  0.6 0.1 pad_maximum_fusion
  0.7 18.0 %attend.1 = (f32[8,144,128]{2,1,0:T(8,128)S(1)}, bf16[128,256,128]{2,1,0:T(8,128)(2,1)}, bf16[128,256,128]{2,1,0:T(8,128)(2,1)}) custom-call(f32[8,128]{1,0:T(8,128)S(1)} %broadcast_in_dim.4.freq_ref, s32[1,128]{1,0:T(1,128)} %bitcast.11, bf16[128,5376]{1,0:T(8,128)(2,1)} %x_hbm.3, f32[42,128]{1,0:T(8,128)} %bitcast.9, bf16[5376,1024]{1,0:T(8,128)(2,1)} %wq_hbm.1, ...), custom_call_target="tpu_custom_call" | custom-call | flops 2818572288 | bytes 38797312 | tf_op jit(solution)/shard_map/attend/pallas_call | solution.py:451
  18.7 38.3 %finish.1 = bf16[128,5376]{1,0:T(8,128)(2,1)S(1)} custom-call(f32[8,144,128]{2,1,0:T(8,128)S(1)} %get-tuple-element.6.o_ref, bf16[1024,5376]{1,0:T(8,128)(2,1)} %wo_hbm.1, bf16[128,5376]{1,0:T(8,128)(2,1)} %x_hbm.3, f32[42,128]{1,0:T(8,128)} %bitcast.10), custom_call_target="tpu_custom_call" | custom-call | flops 176160768 | bytes 11010048 | tf_op jit(solution)/shard_map/finish/pallas_call | solution.py:488
  57.0 1.1 %copy.14 = bf16[128,5376]{1,0:T(8,128)(2,1)} copy(bf16[128,5376]{1,0:T(8,128)(2,1)S(1)} %finish.1) | data formatting | bytes 2752512
  (2 shorter events, 0.0 us)

commit v6 on v4

--- a/solution.py
+++ b/solution.py
@@ -187,50 +187,43 @@
         sent.append(copy)
 
     sign = (1, -1)
-
-    def first(h, d):
-        send((0, 0), h, (d, 0), first_no[h, d])
+    numbers = iter(range(N_GATHER))
+    first_no = {(h, d): next(numbers) for h in (0, 1) for d in (1, -1, 2)}
+    second_no = {(k, h, d): next(numbers) for k in range(RING) for h in (0, 1) for d in ((1, -1, 2) if k == 2 else sign)}
+    forward_no = {(k, h): next(numbers) for k in (0, 1, 3) for h in (0, 1)}
 
     def second(da, h):
-        for d in sign:
+        for d in (2, 1, -1) if da == 2 else sign:
             send((da, 0), h, (0, d), second_no[da % RING, h, d])
 
     def got_second(da, h):
         for d in (sign[h], -sign[h]):
             wait((da, -d), h, second_no[da % RING, h, d])
-            if d == sign[h]:
+            if da != 2 and d == sign[h]:
                 send((da, -d), h, (0, d), forward_no[da % RING, h])
 
     def pairs(da):
         to_pair(da, -1)
         to_pair(da, 1)
 
-    numbers = iter(range(N_GATHER))
-    first_no = {(h, d): next(numbers) for h in (0, 1) for d in sign}
-    diag_no = {h: next(numbers) for h in (0, 1)}
-    second_no = {(k, h, d): next(numbers) for k in range(RING) for h in (0, 1) for d in sign}
-    forward_no = {(k, h): next(numbers) for k in range(RING) for h in (0, 1)}
-
-    for h in (0, 1):
-        first(h, 1)
-        first(h, -1)
+    for h in (0, 1):
+        for d in (2, 1, -1):
+            send((0, 0), h, (d, 0), first_no[h, d])
         second(0, h)
     to_pair(0, 0)
     for h in (0, 1):
         for d in (sign[h], -sign[h]):
             wait((-d, 0), h, first_no[h, d])
-            if d == sign[h]:
-                send((-d, 0), h, (d, 0), diag_no[h])
             second(-d, h)
+    for h in (0, 1):
+        wait((2, 0), h, first_no[h, 2])
+        second(2, h)
     to_pair(-1, 0)
     to_pair(1, 0)
+    to_pair(2, 0)
     for h in (0, 1):
         got_second(0, h)
     pairs(0)
-    for h in (0, 1):
-        wait((2, 0), h, diag_no[h])
-        second(2, h)
-    to_pair(2, 0)
     for h in (0, 1):
         got_second(-1, h)
         got_second(1, h)
@@ -242,10 +235,13 @@
     for h in (0, 1):
         got_second(2, h)
     pairs(2)
-    for k in (-1, 1, 2):
+    for k in (-1, 1):
         for h in (0, 1):
             wait((k, 2), h, forward_no[k % RING, h])
         to_pair(k, 2)
+    for h in (0, 1):
+        wait((2, 2), h, second_no[2, h, 2])
+    to_pair(2, 2)
 
     def from_pair(da, db):
         ref = gath.at[(1 - c) * RING * RING + ((b + da) % RING) * RING + (a + db) % RING]

time: 56.7 us -> 56.2 us (level)
  no operation moved by 1% of the time
where the time goes in v6:
time: 56.2 us; the launch traced here: 56.1 us
  Pallas kernels  54.3 us (97%)
  local copies, waits for them, and re-layouts  1.09 us (2%)
  between operations  0.65 us (1%)
    pallas_call x1, Pallas kernels, finish(): pl.pallas_call(functools.partial(comm_kernel, heads), out_shape=jax.Shape...  36.3 us
    pallas_call x1, Pallas kernels, attend(): pl.pallas_call(functools.partial(attend_kernel, kv_heads), out_shape=(jax...  18 us

profile of v6, /device:TPU:97, one launch (start us, length us, event | category | flops | bytes accessed | tf_op | source)
XLA Modules:
  0.0 56.1 jit_solution(10059312554740894075)
XLA Ops:
  0.6 0.1 pad_maximum_fusion
  0.7 18.0 %attend.1 = (f32[8,144,128]{2,1,0:T(8,128)S(1)}, bf16[128,256,128]{2,1,0:T(8,128)(2,1)}, bf16[128,256,128]{2,1,0:T(8,128)(2,1)}) custom-call(f32[8,128]{1,0:T(8,128)S(1)} %broadcast_in_dim.4.freq_ref, s32[1,128]{1,0:T(1,128)} %bitcast.11, bf16[128,5376]{1,0:T(8,128)(2,1)} %x_hbm.3, f32[42,128]{1,0:T(8,128)} %bitcast.9, bf16[5376,1024]{1,0:T(8,128)(2,1)} %wq_hbm.1, ...), custom_call_target="tpu_custom_call" | custom-call | flops 2818572288 | bytes 38797312 | tf_op jit(solution)/shard_map/attend/pallas_call | solution.py:423
  18.7 36.3 %finish.1 = bf16[128,5376]{1,0:T(8,128)(2,1)S(1)} custom-call(f32[8,144,128]{2,1,0:T(8,128)S(1)} %get-tuple-element.6.o_ref, bf16[1024,5376]{1,0:T(8,128)(2,1)} %wo_hbm.1, bf16[128,5376]{1,0:T(8,128)(2,1)} %x_hbm.3, f32[42,128]{1,0:T(8,128)} %bitcast.10), custom_call_target="tpu_custom_call" | custom-call | flops 176160768 | bytes 11010048 | tf_op jit(solution)/shard_map/finish/pallas_call | solution.py:459
  55.0 1.1 %copy.14 = bf16[128,5376]{1,0:T(8,128)(2,1)} copy(bf16[128,5376]{1,0:T(8,128)(2,1)S(1)} %finish.1) | data formatting | bytes 2752512
  (2 shorter events, 0.0 us)
